TPU v7x, 256 devices: a whole 4x4x8 slice. The times are simulated.
256 devices in a mesh: ctx: 32 (over z, x), tp: 8 (over y, core).
Axes of the slice: x: 4, y: 4, z: 8, core: 2. Of those that a mesh axis runs over, the one named last changes fastest.
Arguments:
- q_nope: bfloat16 [32, 128, 128], P('ctx', 'tp'), may hold values from -6 to 6
- q_rope: bfloat16 [32, 128, 64], P('ctx', 'tp'), may hold values from -256 to 256
- w_uk: bfloat16 [128, 128, 512], P('tp'), may hold values from -0.5 to 0.5
- w_uv: bfloat16 [128, 512, 128], P('tp'), may hold values from -3 to 3
- w_out: bfloat16 [16384, 7168], P('tp', 'ctx'), may hold values from -0.046875 to 0.046875
- prefix_cache: bfloat16 [131072, 576], P('ctx'), may hold values from -6 to 6
- block_table: int32 [2048], P('ctx'), may hold values from 0 to 2047, each once
- prefix_len: int32 [32], replicated, may hold values from 32768 to 131072
- suffix_cache: bfloat16 [32, 256, 576], P('ctx'), may hold values from -12 to 12
- suffix_len: int32 [32], P('ctx'), may hold values from 2 to 256
Outputs:
- layer_out: bfloat16 [32, 7168], P('tp', 'ctx')
Inputs may be any that keep to these rules, and one draw needn't show every extreme that they name: A permutation: slots b * 64 to b * 64 + 63 of prefix_cache hold prefix positions block_table[b] * 64 onwards.
All inputs are finite; a program needn't handle non-finite values.
Results may differ from a plain program's by a relative error of at most 0.0078.
Values may be sent and summed in bfloat16 or wider, within the bound.
No kernel may reach another device: no remote copies, remote signals or barrier semaphores. Data moves between devices by JAX's collectives and lax.ppermute only.
A program may use at most 64 MiB of HBM per device.

v0:
```python
import math

import jax
import jax.numpy as jnp
from jax import lax
from jax.sharding import PartitionSpec as P

LAT = 512
ROPE = 64
NOPE = 128
BLOCK = 64


masked_value = -1e30


def sent_to_all(value, axis):
    length = lax.axis_size(axis)
    return lax.all_to_all(
        jnp.broadcast_to(value[None], (length, *value.shape)), axis, 0, 0, tiled=True
    )


def joined_along(pieces, dim):
    shape = list(pieces.shape[1:])
    shape[dim] *= pieces.shape[0]
    return jnp.moveaxis(pieces, 0, dim).reshape(shape)


def collect(value, axis, dim):
    pieces = sent_to_all(value, axis)
    return joined_along(pieces, dim)


def in_one_piece(arrays, axis, split_dim, concat_dim, along):
    widths = [math.prod(a.shape[along:]) for a in arrays]
    both = jnp.concatenate(
        [a.reshape(*a.shape[:along], w) for a, w in zip(arrays, widths)], axis=along
    )
    out = lax.all_to_all(both, axis, split_axis=split_dim, concat_axis=concat_dim, tiled=True)
    pieces = jnp.split(out, [sum(widths[:k]) for k in range(1, len(widths))], axis=along)
    return tuple((b.reshape(*out.shape[:along], *a.shape[along:]) for a, b in zip(arrays, pieces)))


def split_up(value, dim, length):
    shape = value.shape
    pieces = value.reshape(*shape[:dim], length, shape[dim] // length, *shape[dim + 1 :])
    return jnp.moveaxis(pieces, dim, 0)


def sent_and_summed(value, axis, dim):
    pieces = split_up(value, dim, lax.axis_size(axis))
    arrived = lax.all_to_all(pieces, axis, split_axis=0, concat_axis=0, tiled=True)
    return arrived.sum(axis=0)


def partial_stats(scores, visible, values, pattern):
    row_peak = jnp.max(jnp.where(visible, scores, masked_value), axis=2)
    weights = jnp.where(visible, jnp.exp(scores - row_peak[:, :, None]), 0.0).astype(jnp.bfloat16)
    row_mass = jnp.sum(weights, axis=2, dtype=jnp.float32)
    row_weighted = jnp.einsum(pattern, weights, values, preferred_element_type=jnp.float32)
    return (row_peak, row_mass, row_weighted)


def value_project(latent, value_weight):
    return jnp.einsum("rhc,hcv->rhv", latent, value_weight)


def on_device(
    q_nope,
    q_rope,
    w_uk,
    w_uv,
    w_out,
    prefix_cache,
    block_table,
    prefix_len,
    suffix_cache,
    suffix_len,
):
    softmax_scale = (NOPE + ROPE) ** (-0.5)
    q_latent = jnp.einsum("rhn,hnc->rhc", q_nope, w_uk, preferred_element_type=jnp.float32).astype(
        jnp.bfloat16
    )
    own_queries = jnp.concatenate([q_latent, q_rope], axis=2)
    all_queries = collect(own_queries, "ctx", 0)
    ctx_count = lax.axis_size("ctx")
    own_count = own_queries.shape[0]
    value_weight = w_uv.astype(jnp.float32)
    positions = (
        block_table[:, None] * BLOCK + jnp.arange(BLOCK, dtype=jnp.int32)[None, :]
    ).reshape(-1)
    visible = (positions[None, :] < prefix_len[:, None])[:, None, :]
    scores = (
        jnp.einsum("rhc,tc->rht", all_queries, prefix_cache, preferred_element_type=jnp.float32)
        * softmax_scale
    )
    row_peak, row_mass, row_weighted = partial_stats(
        scores, visible, prefix_cache[:, :LAT], "rht,tc->rhc"
    )
    suffix_scores = (
        jnp.einsum("rhc,rtc->rht", own_queries, suffix_cache, preferred_element_type=jnp.float32)
        * softmax_scale
    )
    suffix_slots = jnp.arange(suffix_cache.shape[1], dtype=jnp.int32)
    suffix_visible = (suffix_slots[None, :] < suffix_len[:, None])[:, None, :]
    tail_peak, tail_mass, tail_weighted = partial_stats(
        suffix_scores, suffix_visible, suffix_cache[:, :, :LAT], "rht,rtc->rhc"
    )

    def by_owner(values):
        return values.reshape((ctx_count, own_count) + values.shape[1:])

    got_peak, got_mass, got_weighted = in_one_piece(
        (by_owner(row_peak), by_owner(row_mass), by_owner(row_weighted)), "ctx", 0, 0, 3
    )
    highest = jnp.maximum(jnp.max(got_peak, axis=0), tail_peak)
    factors = jnp.exp(got_peak - highest[None])
    tail_factor = jnp.exp(tail_peak - highest)
    total_mass = jnp.sum(factors * got_mass, axis=0) + tail_factor * tail_mass
    total_weighted = (
        jnp.sum(factors[..., None] * got_weighted, axis=0) + tail_factor[:, :, None] * tail_weighted
    )
    head_values = value_project(total_weighted / total_mass[:, :, None], value_weight).astype(
        jnp.bfloat16
    )
    flat_values = head_values.reshape(own_count, -1)
    every_value = collect(flat_values, "ctx", 0)
    return sent_and_summed(
        jnp.dot(every_value, w_out, preferred_element_type=jnp.float32), "tp", 0
    ).astype(jnp.bfloat16)


def solution(mesh):
    placed = (
        P("ctx", "tp", None),
        P("ctx", "tp", None),
        P("tp", None, None),
        P("tp", None, None),
        P("tp", "ctx"),
        P("ctx", None),
        P("ctx"),
        P(),
        P("ctx", None, None),
        P("ctx"),
    )
    return jax.shard_map(
        on_device, mesh=mesh, in_specs=placed, out_specs=P("tp", "ctx"), check_vma=False
    )
```

profile of v0, /device:TPU:1, one launch (start us, length us, event | category | flops | bytes accessed | tf_op | source)
XLA Modules:
  0.0 127.9 jit_solution(11942779470466033778)
XLA Ops:
  0.0 0.0 copy-start
  0.0 1.6 %copy-done = bf16[16,128,512]{2,1,0:T(8,128)(2,1)S(1)} copy-done((bf16[16,128,512]{2,1,0:T(8,128)(2,1)S(1)}, bf16[16,128,512]{2,1,0:T(8,128)(2,1)}, u32[]{:S(2)}) %copy-start) | copy-done | bytes 2097176
  1.6 1.1 fusion.23
  2.7 0.7 maximum_bitcast_fusion.1
  3.4 0.9 broadcast_in_dim.66
  4.3 11.9 %all-to-all-start = ((bf16[32,1,16,576]{3,2,1,0:T(8,128)(2,1)}), bf16[32,1,16,576]{3,2,1,0:T(8,128)(2,1)S(1)}, u32[]{:S(2)}, u32[]{:S(2)}) async-start(bf16[32,1,16,576]{3,2,1,0:T(8,128)(2,1)} %broadcast_in_dim.66), calls=%async_computation | async-start | bytes 1310720 | tf_op jit(solution)/shard_map/all_to_all | solution.py:19
  16.1 0.7 broadcast_multiply_fusion
  16.8 0.1 iota_add_fusion
  16.9 0.1 add.36
  16.9 0.8 broadcast_compare_fusion
  17.7 17.1 %all-to-all-done = bf16[32,1,16,576]{3,2,1,0:T(8,128)(2,1)S(1)} async-done(((bf16[32,1,16,576]{3,2,1,0:T(8,128)(2,1)}), bf16[32,1,16,576]{3,2,1,0:T(8,128)(2,1)S(1)}, u32[]{:S(2)}, u32[]{:S(2)}) %all-to-all-start) | async-done | bytes 589856 | tf_op jit(solution)/shard_map/all_to_all | solution.py:19
  34.8 5.9 %select_reduce_fusion = (f32[32,16]{1,0:T(8,128)S(1)}, f32[32,16,4096]{2,1,0:T(8,128)S(1)}) fusion(pred[32,4096]{1,0:T(8,128)(4,1)S(1)} %broadcast_compare_fusion, bf16[4096,576]{0,1:T(8,128)(2,1)} %param.15, bf16[32,1,16,576]{3,2,1,0:T(8,128)(2,1)S(1)} %all-to-all-done), kind=kOutput, calls=%fused_computation.2 | convolution fusion | flops 2422210048 | bytes 13830144 | tf_op jit(solution)/shard_map/rhc,tc->rht/dot_general | solution.py:95
  40.7 4.6 %fusion.5 = f32[32,1,16,512]{3,2,0,1:T(8,128)S(1)} fusion(bf16[4096,576]{0,1:T(8,128)(2,1)} %param.15, f32[32,16,4096]{2,1,0:T(8,128)S(1)} %get-tuple-element.11, f32[32,16]{1,0:T(8,128)S(1)} %get-tuple-element.10, pred[32,4096]{1,0:T(8,128)(4,1)S(1)} %broadcast_compare_fusion), kind=kOutput, calls=%fused_computation.8 | convolution fusion | flops 2155872256 | bytes 13764608 | tf_op jit(solution)/shard_map/rht,tc->rhc/dot_general | solution.py:61
  45.3 2.4 %convert_reduce_fusion = f32[32,16]{1,0:T(8,128)S(1)} fusion(f32[32,16]{1,0:T(8,128)S(1)} %get-tuple-element.10, f32[32,16,4096]{2,1,0:T(8,128)S(1)} %get-tuple-element.11, pred[32,4096]{1,0:T(8,128)(4,1)S(1)} %broadcast_compare_fusion), kind=kLoop, calls=%fused_computation | loop fusion | flops 12582400 | bytes 8523776 | tf_op jit(solution)/shard_map/reduce_sum | solution.py:60
  47.7 0.0 copy-start.1
  47.7 0.3 copy.32
  48.0 1.0 copy.31
  49.0 2.6 %maximum_bitcast_fusion = f32[32,1,16,514]{3,2,1,0:T(8,128)} fusion(f32[32,1,16,512]{3,2,0,1:T(8,128)S(1)} %fusion.5, f32[32,1,16,1]{3,2,0,1:T(8,128)S(1)} %copy.32, f32[32,1,16,1]{3,2,0,1:T(8,128)} %copy.31), kind=kLoop, calls=%fused_computation.9 | loop fusion | flops 526336 | bytes 2105344 | tf_op jit(solution)/shard_map/concatenate | solution.py:37
  51.5 5.5 %all-to-all-start.1 = ((f32[32,1,16,514]{3,2,1,0:T(8,128)}), f32[32,1,16,514]{3,2,1,0:T(8,128)S(1)}, u32[]{:S(2)}, u32[]{:S(2)}) async-start(f32[32,1,16,514]{3,2,1,0:T(8,128)} %maximum_bitcast_fusion), calls=%async_computation.1 | async-start | bytes 2621440 | tf_op jit(solution)/shard_map/all_to_all | solution.py:40
  57.7 0.0 copy-done.1
  57.7 1.2 select_reduce_fusion.1
  59.0 0.2 convert_reduce_fusion.1
  59.2 28.8 %all-to-all-done.1 = f32[32,1,16,514]{3,2,1,0:T(8,128)S(1)} async-done(((f32[32,1,16,514]{3,2,1,0:T(8,128)}), f32[32,1,16,514]{3,2,1,0:T(8,128)S(1)}, u32[]{:S(2)}, u32[]{:S(2)}) %all-to-all-start.1) | async-done | bytes 1052704 | tf_op jit(solution)/shard_map/all_to_all | solution.py:40
  87.9 1.0 fusion.27
  88.9 1.1 copy.47
  90.1 0.1 exponential_bitcast_fusion
  90.1 0.1 copy.35
  90.2 1.1 copy.48
  91.3 0.2 fusion.21
  91.5 0.4 fusion.11
  92.0 0.0 copy-start.2
  92.0 1.2 fusion.10
  93.2 2.0 %fusion.18 = f32[16,1,128]{2,1,0:T(1,128)S(1)} fusion(bf16[16,512,128]{2,1,0:T(8,128)(2,1)} %param.13, bf16[16,512,1]{1,0,2:T(8,128)(2,1)S(1)} %fusion.10), kind=kOutput, calls=%fused_computation.25 | convolution fusion | flops 2097152 | bytes 2121728 | tf_op jit(solution)/shard_map/rhc,hcv->rhv/dot_general | solution.py:66
  95.2 0.1 broadcast_in_dim.73
  95.4 0.5 broadcast.66
  95.9 1.4 %reduce.9 = bf16[32,2048]{1,0:T(8,128)(2,1)S(1)} reduce(bf16[32,1,2048]{2,1,0:T(2,128)(2,1)S(1)} %broadcast_in_dim.73, bf16[]{:T(256)} %broadcast.66), dimensions={1}, to_apply=%broadcast_in_dim.73.reduce_sub_computation | reduce | bytes 262146 | tf_op jit(solution)/shard_map/broadcast_in_dim | solution.py:20
  97.3 0.1 reshape.236
  97.3 16.1 %all_to_all.20 = bf16[32,2,1024]{2,1,0:T(2,128)(2,1)S(1)} all-to-all(bf16[32,2,1024]{2,1,0:T(2,128)(2,1)S(1)} %reshape.236), channel_id=1, replica_groups=mesh['ctx'=32,'tp'=8] {'ctx'}, dimensions={0} | all-to-all | bytes 262144 | tf_op jit(solution)/shard_map/all_to_all | solution.py:19
  113.4 0.1 reshape.237
  113.5 0.7 reduce.8
  114.2 0.1 dot_general.29
  114.3 0.0 copy-done.2
  114.3 0.4 fusion.12
  114.7 12.6 %all_to_all.21 = f32[8,4,224]{2,1,0:T(4,128)S(1)} all-to-all(f32[8,4,224]{2,1,0:T(4,128)S(1)} %fusion.12), channel_id=1, replica_groups=mesh['ctx'=32,'tp'=8] {'tp'}, dimensions={0} | all-to-all | bytes 57344 | tf_op jit(solution)/shard_map/all_to_all | solution.py:53
  127.3 0.6 reduce_sum.49
  (5 shorter events, 0.0 us)
Async XLA Ops:
  0.0 1.6 %copy-start = (bf16[16,128,512]{2,1,0:T(8,128)(2,1)S(1)}, bf16[16,128,512]{2,1,0:T(8,128)(2,1)}, u32[]{:S(2)}) copy-start(bf16[16,128,512]{2,1,0:T(8,128)(2,1)} %param.12) | copy-start | bytes 6291460
  4.3 30.5 %all-to-all-start = ((bf16[32,1,16,576]{3,2,1,0:T(8,128)(2,1)}), bf16[32,1,16,576]{3,2,1,0:T(8,128)(2,1)S(1)}, u32[]{:S(2)}, u32[]{:S(2)}) async-start(bf16[32,1,16,576]{3,2,1,0:T(8,128)(2,1)} %broadcast_in_dim.66), calls=%async_computation | async-start | bytes 1310720 | tf_op jit(solution)/shard_map/all_to_all | solution.py:19
  47.7 10.0 %copy-start.1 = (bf16[1,16,64]{2,1,0:T(8,128)(2,1)S(1)}, bf16[1,16,64]{2,1,0:T(8,128)(2,1)}, u32[]{:S(2)}) copy-start(bf16[1,16,64]{2,1,0:T(8,128)(2,1)} %param.11) | copy-start | bytes 6148
  51.5 36.4 %all-to-all-start.1 = ((f32[32,1,16,514]{3,2,1,0:T(8,128)}), f32[32,1,16,514]{3,2,1,0:T(8,128)S(1)}, u32[]{:S(2)}, u32[]{:S(2)}) async-start(f32[32,1,16,514]{3,2,1,0:T(8,128)} %maximum_bitcast_fusion), calls=%async_computation.1 | async-start | bytes 2621440 | tf_op jit(solution)/shard_map/all_to_all | solution.py:40
  92.0 22.3 %copy-start.2 = (bf16[2048,224]{0,1:T(8,128)(2,1)S(1)}, bf16[2048,224]{0,1:T(8,128)(2,1)}, u32[]{:S(2)}) copy-start(bf16[2048,224]{0,1:T(8,128)(2,1)} %param.14) | copy-start | bytes 2752516
where the time goes:
time: 129 us; the launch traced here: 128 us
  waiting for transfers between devices  45.8 us (36%)
  blocking collectives  28.7 us (22%)
  starting transfers between devices  17.4 us (13%)
  matrix products  16.3 us (13%)
  other arithmetic  11.8 us (9%)
  local copies, waits for them, and re-layouts  7.07 us (5%)
    all_to_all x1, waiting for transfers between devices, in_one_piece(): lax.all_to_all(both, axis, split_axis=split_dim, concat_axis=concat_dim,...  28.8 us
    all_to_all x1, waiting for transfers between devices, sent_to_all(): lax.all_to_all(jnp.broadcast_to(value[None], (length, *value.shape)), axi...  17.1 us
    all_to_all x1, blocking collectives, sent_to_all(): lax.all_to_all(jnp.broadcast_to(value[None], (length, *value.shape)), axi...  16.1 us
    all_to_all x1, blocking collectives, sent_and_summed(): lax.all_to_all(pieces, axis, split_axis=0, concat_axis=0, tiled=True)  12.6 us
    all_to_all x1, starting transfers between devices, sent_to_all(): lax.all_to_all(jnp.broadcast_to(value[None], (length, *value.shape)), axi...  11.9 us
    dot_general x1, matrix products, on_device(): jnp.einsum('rhc,tc->rht', all_queries, prefix_cache, preferred_element_ty...  5.89 us
    dot_general x2, matrix products, partial_stats(): jnp.einsum(pattern, weights, values, preferred_element_type=jnp.float32)  5.8 us
    all_to_all x1, starting transfers between devices, in_one_piece(): lax.all_to_all(both, axis, split_axis=split_dim, concat_axis=concat_dim,...  5.53 us
  transfers between devices with their start and end apart: 2, of which 2 were waited for; matrix products, arithmetic and copies ran while one was open for 2% of the time, Pallas kernels for 0%

commit v1 on v0

--- a/solution.py
+++ b/solution.py
@@ -63,7 +63,10 @@
 
 
 def value_project(latent, value_weight):
-    return jnp.einsum("rhc,hcv->rhv", latent, value_weight)
+    high = latent.astype(jnp.bfloat16)
+    low = (latent - high.astype(jnp.float32)).astype(jnp.bfloat16)
+    parts = jnp.stack([high, low])
+    return jnp.einsum("prhc,hcv->prhv", parts, value_weight, preferred_element_type=jnp.float32).sum(axis=0)
 
 
 def on_device(
@@ -79,14 +82,16 @@
     suffix_len,
 ):
     softmax_scale = (NOPE + ROPE) ** (-0.5)
-    q_latent = jnp.einsum("rhn,hnc->rhc", q_nope, w_uk, preferred_element_type=jnp.float32).astype(
-        jnp.bfloat16
-    )
-    own_queries = jnp.concatenate([q_latent, q_rope], axis=2)
-    all_queries = collect(own_queries, "ctx", 0)
+    raw_queries = collect(jnp.concatenate([q_nope, q_rope], axis=2), "ctx", 0)
+
+    def absorb(nope, rope):
+        latent = jnp.einsum("rhn,hnc->rhc", nope, w_uk, preferred_element_type=jnp.float32)
+        return jnp.concatenate([latent.astype(jnp.bfloat16), rope], axis=2)
+
+    own_queries = absorb(q_nope, q_rope)
+    all_queries = absorb(raw_queries[:, :, :NOPE], raw_queries[:, :, NOPE:])
     ctx_count = lax.axis_size("ctx")
     own_count = own_queries.shape[0]
-    value_weight = w_uv.astype(jnp.float32)
     positions = (
         block_table[:, None] * BLOCK + jnp.arange(BLOCK, dtype=jnp.int32)[None, :]
     ).reshape(-1)
@@ -98,6 +103,7 @@
     row_peak, row_mass, row_weighted = partial_stats(
         scores, visible, prefix_cache[:, :LAT], "rht,tc->rhc"
     )
+    row_weighted = value_project(row_weighted, w_uv)
     suffix_scores = (
         jnp.einsum("rhc,rtc->rht", own_queries, suffix_cache, preferred_element_type=jnp.float32)
         * softmax_scale
@@ -107,6 +113,7 @@
     tail_peak, tail_mass, tail_weighted = partial_stats(
         suffix_scores, suffix_visible, suffix_cache[:, :, :LAT], "rht,rtc->rhc"
     )
+    tail_weighted = value_project(tail_weighted, w_uv)
 
     def by_owner(values):
         return values.reshape((ctx_count, own_count) + values.shape[1:])
@@ -121,9 +128,7 @@
     total_weighted = (
         jnp.sum(factors[..., None] * got_weighted, axis=0) + tail_factor[:, :, None] * tail_weighted
     )
-    head_values = value_project(total_weighted / total_mass[:, :, None], value_weight).astype(
-        jnp.bfloat16
-    )
+    head_values = (total_weighted / total_mass[:, :, None]).astype(jnp.bfloat16)
     flat_values = head_values.reshape(own_count, -1)
     every_value = collect(flat_values, "ctx", 0)
     return sent_and_summed(

time: 129 us -> 93.9 us (0.73)
  waiting for transfers between devices: 45.8 us -> 19.5 us
  local copies, waits for them, and re-layouts: 7.07 us -> 4.86 us
  other arithmetic: 11.8 us -> 9.79 us
  matrix products: 16.3 us -> 14.3 us
  blocking collectives: 28.7 us -> 27.4 us
    all_to_all x1, waiting for transfers between devices: 28.8 us -> 12.8 us  [in_one_piece(): lax.all_to_all(both, axis, split_axis=split_dim, concat_axis=concat_dim,...]
    all_to_all x1, waiting for transfers between devices: 17.1 us -> 6.69 us  [sent_to_all(): lax.all_to_all(jnp.broadcast_to(value[None], (length, *value.shape)), axi...]
    dot_general x2, matrix products: 5.8 us -> 2.65 us  [partial_stats(): jnp.einsum(pattern, weights, values, preferred_element_type=jnp.float32)]
    dot_general x1, matrix products: 5.89 us -> 4.05 us  [on_device(): jnp.einsum('rhc,tc->rht', all_queries, prefix_cache, preferred_element_ty...]
    dot_general x2 -> x4, matrix products: 3.04 us -> 4.76 us  [the longest x2 3.29 us: value_project(): jnp.einsum('prhc,hcv->prhv', parts, value_weight, preferred_element_type=...]
    unnamed x10 -> x12, local copies, waits for them, and re-layouts: 4.04 us -> 2.33 us
    concatenate x1, other arithmetic: 2.55 us -> 1.13 us  [in_one_piece(): jnp.concatenate([a.reshape(*a.shape[:along], w) for a, w in zip(arrays, w...]
  transfers between devices with their start and end apart: 2 -> 2, of which waited for: 2 -> 2; matrix products, arithmetic and copies ran while one was open for 2% -> 7% of each run, Pallas kernels for 0% -> 0%
where the time goes in v1:
time: 93.9 us; the launch traced here: 93.4 us
  blocking collectives  27.4 us (29%)
  waiting for transfers between devices  19.5 us (21%)
  starting transfers between devices  16.7 us (18%)
  matrix products  14.3 us (15%)
  other arithmetic  9.79 us (10%)
  local copies, waits for them, and re-layouts  4.86 us (5%)
    all_to_all x1, blocking collectives, sent_to_all(): lax.all_to_all(jnp.broadcast_to(value[None], (length, *value.shape)), axi...  15.1 us
    all_to_all x1, waiting for transfers between devices, in_one_piece(): lax.all_to_all(both, axis, split_axis=split_dim, concat_axis=concat_dim,...  12.8 us
    all_to_all x1, blocking collectives, sent_and_summed(): lax.all_to_all(pieces, axis, split_axis=0, concat_axis=0, tiled=True)  12.3 us
    all_to_all x1, starting transfers between devices, sent_to_all(): lax.all_to_all(jnp.broadcast_to(value[None], (length, *value.shape)), axi...  11.9 us
    all_to_all x1, waiting for transfers between devices, sent_to_all(): lax.all_to_all(jnp.broadcast_to(value[None], (length, *value.shape)), axi...  6.69 us
    all_to_all x1, starting transfers between devices, in_one_piece(): lax.all_to_all(both, axis, split_axis=split_dim, concat_axis=concat_dim,...  4.88 us
    dot_general x1, matrix products, on_device(): jnp.einsum('rhc,tc->rht', all_queries, prefix_cache, preferred_element_ty...  4.05 us
    dot_general x2, matrix products, value_project(): jnp.einsum('prhc,hcv->prhv', parts, value_weight, preferred_element_type=...  3.29 us
  transfers between devices with their start and end apart: 2, of which 2 were waited for; matrix products, arithmetic and copies ran while one was open for 7% of the time, Pallas kernels for 0%

profile of v1, /device:TPU:1, one launch (start us, length us, event | category | flops | bytes accessed | tf_op | source)
XLA Modules:
  0.0 93.4 jit_solution(15275648361208070045)
XLA Ops:
  0.0 0.0 copy-start
  0.0 0.9 maximum_bitcast_fusion.3
  0.9 0.7 broadcast_in_dim.64
  1.6 11.9 %all-to-all-start = ((bf16[32,1,16,192]{3,2,1,0:T(8,128)(2,1)}), bf16[32,1,16,192]{3,2,1,0:T(8,128)(2,1)S(1)}, u32[]{:S(2)}, u32[]{:S(2)}) async-start(bf16[32,1,16,192]{3,2,1,0:T(8,128)(2,1)} %broadcast_in_dim.64), calls=%async_computation | async-start | bytes 524288 | tf_op jit(solution)/shard_map/all_to_all | solution.py:19
  13.4 0.7 broadcast_multiply_fusion
  14.1 0.1 iota_add_fusion
  14.2 0.1 add.38
  14.2 0.8 broadcast_compare_fusion
  15.0 0.0 copy-done
  15.1 1.1 %fusion.32 = bf16[16,1,512]{2,1,0:T(2,128)(2,1)S(1)} fusion(bf16[16,128,512]{2,1,0:T(8,128)(2,1)S(1)} %copy-done, bf16[16,128,1]{1,0,2:T(8,128)(2,1)} %bitcast.104), kind=kOutput, calls=%fused_computation.56 | convolution fusion | flops 2097152 | bytes 2117632 | tf_op jit(solution)/shard_map/rhn,hnc->rhc/dot_general | solution.py:88
  16.8 1.2 %select_reduce_fusion.1 = (f32[16]{0:T(128)S(1)}, f32[16,256]{1,0:T(8,128)S(1)}) fusion(pred[256]{0:T(512)(128)(4,1)S(1)} %iota_compare_fusion, bf16[1,256,576]{1,2,0:T(8,128)(2,1)} %param.18, bf16[1,16,64]{2,1,0:T(8,128)(2,1)} %param.11, bf16[1,16,512]{2,1,0:T(8,128)(2,1)S(1)} %bitcast.103), kind=kOutput, calls=%fused_computation.46 | convolution fusion | flops 4767728 | bytes 330048 | tf_op jit(solution)/shard_map/rhc,rtc->rht/dot_general | solution.py:108
  18.1 6.7 %all-to-all-done = bf16[32,1,16,192]{3,2,1,0:T(8,128)(2,1)S(1)} async-done(((bf16[32,1,16,192]{3,2,1,0:T(8,128)(2,1)}), bf16[32,1,16,192]{3,2,1,0:T(8,128)(2,1)S(1)}, u32[]{:S(2)}, u32[]{:S(2)}) %all-to-all-start) | async-done | bytes 196640 | tf_op jit(solution)/shard_map/all_to_all | solution.py:19
  24.7 0.0 copy-start.3
  24.7 0.1 copy.70
  24.9 0.4 fusion.7
  25.3 0.1 pad_maximum_fusion.1
  25.3 1.7 %copy-done.3 = bf16[4096,576]{0,1:T(8,128)(2,1)S(1)} copy-done((bf16[4096,576]{0,1:T(8,128)(2,1)S(1)}, bf16[4096,576]{0,1:T(8,128)(2,1)}, u32[]{:S(2)}) %copy-start.3) | copy-done | bytes 4718616
  27.1 4.1 %select_reduce_fusion = (f32[32,16]{1,0:T(8,128)S(1)}, f32[32,16,4096]{2,1,0:T(8,128)S(1)}) fusion(pred[32,4096]{1,0:T(8,128)(4,1)S(1)} %broadcast_compare_fusion, bf16[4096,576]{0,1:T(8,128)(2,1)S(1)} %copy-done.3, bf16[32,16,576]{2,0,1:T(8,128)(2,1)S(1)} %pad_maximum_fusion.1), kind=kOutput, calls=%fused_computation.2 | convolution fusion | flops 2422210048 | bytes 13830144 | tf_op jit(solution)/shard_map/rhc,tc->rht/dot_general | solution.py:100
  31.1 2.5 %convert_reduce_fusion = f32[32,16]{1,0:T(8,128)S(1)} fusion(f32[32,16]{1,0:T(8,128)S(1)} %get-tuple-element.14, f32[32,16,4096]{2,1,0:T(8,128)S(1)} %get-tuple-element.15, pred[32,4096]{1,0:T(8,128)(4,1)S(1)} %broadcast_compare_fusion), kind=kLoop, calls=%fused_computation | loop fusion | flops 12582400 | bytes 8523776 | tf_op jit(solution)/shard_map/reduce_sum | solution.py:60
  33.6 0.0 copy-start.1
  33.7 2.5 %convert_bitcast_fusion = (bf16[1,32,16,512]{3,2,1,0:T(8,128)(2,1)S(1)}, bf16[1,32,16,512]{3,2,1,0:T(8,128)(2,1)S(1)}) fusion(bf16[4096,576]{0,1:T(8,128)(2,1)S(1)} %copy-done.3, f32[32,16,4096]{2,1,0:T(8,128)S(1)} %get-tuple-element.15, f32[32,16]{1,0:T(8,128)S(1)} %get-tuple-element.14, pred[32,4096]{1,0:T(8,128)(4,1)S(1)} %broadcast_compare_fusion), kind=kOutput, calls=%fused_computation.31 | convolution fusion | flops 2156920832 | bytes 13778944 | tf_op jit(solution)/shard_map/rht,tc->rhc/dot_general | solution.py:61
  36.1 0.0 copy-start.2
  36.1 0.1 pad_maximum_fusion
  36.2 0.0 copy-done.1
  36.3 1.3 %fusion.8 = f32[16,32,128]{2,1,0:T(8,128)S(1)} fusion(bf16[16,512,128]{2,1,0:T(8,128)(2,1)S(1)} %copy-done.1, bf16[2,32,16,512]{3,2,1,0:T(8,128)(2,1)S(1)} %pad_maximum_fusion), kind=kOutput, calls=%fused_computation.12 | convolution fusion | flops 134283264 | bytes 3407872 | tf_op jit(solution)/shard_map/prhc,hcv->prhv/dot_general | solution.py:69
  37.6 0.2 copy.40
  37.7 0.3 copy.39
  38.0 0.3 copy.38
  38.3 1.1 %pad_maximum_fusion.2 = f32[32,1,16,130]{3,2,1,0:T(8,128)} fusion(f32[32,1,16,128]{3,2,1,0:T(8,128)S(1)} %copy.40, f32[32,1,16,1]{3,2,1,0:T(8,128)S(1)} %copy.39, f32[32,1,16,1]{3,2,1,0:T(8,128)S(1)} %copy.38), kind=kLoop, calls=%fused_computation.23 | loop fusion | flops 133120 | bytes 532480 | tf_op jit(solution)/shard_map/concatenate | solution.py:37
  39.4 4.9 %all-to-all-start.1 = ((f32[32,1,16,130]{3,2,1,0:T(8,128)}), f32[32,1,16,130]{3,2,1,0:T(8,128)S(1)}, u32[]{:S(2)}, u32[]{:S(2)}) async-start(f32[32,1,16,130]{3,2,1,0:T(8,128)} %pad_maximum_fusion.2), calls=%async_computation.1 | async-start | bytes 1048576 | tf_op jit(solution)/shard_map/all_to_all | solution.py:40
  44.3 0.0 copy-done.2
  44.3 0.2 convert_bitcast_fusion.1
  44.5 0.2 convert_reduce_fusion.1
  44.7 2.0 %convolution_reduce_fusion = f32[16,128]{1,0:T(8,128)S(1)} fusion(bf16[16,512,128]{2,1,0:T(8,128)(2,1)} %param.13, bf16[2,16,512]{2,1,0:T(8,128)(2,1)S(1)} %maximum_bitcast_fusion), kind=kOutput, calls=%fused_computation.14 | convolution fusion | flops 4196352 | bytes 2138112 | tf_op jit(solution)/shard_map/prhc,hcv->prhv/dot_general | solution.py:69
  46.7 12.8 %all-to-all-done.1 = f32[32,1,16,130]{3,2,1,0:T(8,128)S(1)} async-done(((f32[32,1,16,130]{3,2,1,0:T(8,128)}), f32[32,1,16,130]{3,2,1,0:T(8,128)S(1)}, u32[]{:S(2)}, u32[]{:S(2)}) %all-to-all-start.1) | async-done | bytes 266272 | tf_op jit(solution)/shard_map/all_to_all | solution.py:40
  59.5 0.2 slice_reduce_fusion
  59.7 0.2 copy.53
  59.9 0.1 exponential_bitcast_fusion
  59.9 0.1 copy.42
  60.0 0.2 copy.54
  60.2 0.2 fusion.27
  60.4 0.2 fusion.17
  60.6 0.1 div.13
  60.7 0.1 mul.72
  60.8 0.1 broadcast_in_dim.70
  61.0 0.5 broadcast.72
  61.5 1.4 %reduce.14 = bf16[32,2048]{1,0:T(8,128)(2,1)S(1)} reduce(bf16[32,1,2048]{2,1,0:T(2,128)(2,1)S(1)} %broadcast_in_dim.70, bf16[]{:T(256)} %broadcast.72), dimensions={1}, to_apply=%broadcast_in_dim.70.reduce_sub_computation | reduce | bytes 262146 | tf_op jit(solution)/shard_map/broadcast_in_dim | solution.py:20
  62.9 0.1 reshape.257
  62.9 15.1 %all_to_all.20 = bf16[32,2,1024]{2,1,0:T(2,128)(2,1)S(1)} all-to-all(bf16[32,2,1024]{2,1,0:T(2,128)(2,1)S(1)} %reshape.257), channel_id=1, replica_groups=mesh['ctx'=32,'tp'=8] {'ctx'}, dimensions={0} | all-to-all | bytes 262144 | tf_op jit(solution)/shard_map/all_to_all | solution.py:19
  78.1 0.1 reshape.258
  78.2 0.7 reduce.13
  78.9 0.1 dot_general.37
  79.0 1.6 %fusion.12 = f32[8,4,224]{2,1,0:T(4,128)S(1)} fusion(bf16[8,4,2048]{2,1,0:T(4,128)(2,1)S(1)} %dot_general.37, bf16[2048,224]{0,1:T(8,128)(2,1)} %param.14), kind=kOutput, calls=%fused_computation.18 | convolution fusion | flops 29360128 | bytes 1077248 | tf_op jit(solution)/shard_map/dot_general | solution.py:135
  80.5 12.3 %all_to_all.21 = f32[8,4,224]{2,1,0:T(4,128)S(1)} all-to-all(f32[8,4,224]{2,1,0:T(4,128)S(1)} %fusion.12), channel_id=1, replica_groups=mesh['ctx'=32,'tp'=8] {'tp'}, dimensions={0} | all-to-all | bytes 57344 | tf_op jit(solution)/shard_map/all_to_all | solution.py:53
  92.8 0.6 reduce_sum.78
  (7 shorter events, 0.1 us)
Async XLA Ops:
  0.0 15.0 %copy-start = (bf16[16,128,512]{2,1,0:T(8,128)(2,1)S(1)}, bf16[16,128,512]{2,1,0:T(8,128)(2,1)}, u32[]{:S(2)}) copy-start(bf16[16,128,512]{2,1,0:T(8,128)(2,1)} %param.12) | copy-start | bytes 6291460
  1.6 23.2 %all-to-all-start = ((bf16[32,1,16,192]{3,2,1,0:T(8,128)(2,1)}), bf16[32,1,16,192]{3,2,1,0:T(8,128)(2,1)S(1)}, u32[]{:S(2)}, u32[]{:S(2)}) async-start(bf16[32,1,16,192]{3,2,1,0:T(8,128)(2,1)} %broadcast_in_dim.64), calls=%async_computation | async-start | bytes 524288 | tf_op jit(solution)/shard_map/all_to_all | solution.py:19
  24.7 2.3 %copy-start.3 = (bf16[4096,576]{0,1:T(8,128)(2,1)S(1)}, bf16[4096,576]{0,1:T(8,128)(2,1)}, u32[]{:S(2)}) copy-start(bf16[4096,576]{0,1:T(8,128)(2,1)} %param.15) | copy-start | bytes 14155780
  33.6 2.6 %copy-start.1 = (bf16[16,512,128]{2,1,0:T(8,128)(2,1)S(1)}, bf16[16,512,128]{2,1,0:T(8,128)(2,1)}, u32[]{:S(2)}) copy-start(bf16[16,512,128]{2,1,0:T(8,128)(2,1)} %param.13) | copy-start | bytes 6291460
  36.1 8.1 %copy-start.2 = (bf16[1,256,576]{1,2,0:T(8,128)(2,1)S(1)}, bf16[1,256,576]{1,2,0:T(8,128)(2,1)}, u32[]{:S(2)}) copy-start(bf16[1,256,576]{1,2,0:T(8,128)(2,1)} %param.18) | copy-start | bytes 884740
  39.4 20.1 %all-to-all-start.1 = ((f32[32,1,16,130]{3,2,1,0:T(8,128)}), f32[32,1,16,130]{3,2,1,0:T(8,128)S(1)}, u32[]{:S(2)}, u32[]{:S(2)}) async-start(f32[32,1,16,130]{3,2,1,0:T(8,128)} %pad_maximum_fusion.2), calls=%async_computation.1 | async-start | bytes 1048576 | tf_op jit(solution)/shard_map/all_to_all | solution.py:40

commit v2 on v0

v2 whole, which is shorter than its diff:
```python
import functools
import math

import jax
import jax.numpy as jnp
from jax import lax
from jax.experimental import pallas as pl
from jax.experimental.pallas import tpu as pltpu
from jax.sharding import PartitionSpec as P

LAT = 512
ROPE = 64
NOPE = 128
BLOCK = 64
LANES = 128
ROWS = 24
NEG = -1e30
LOG2E = math.log2(math.e)


def segment_kernel(q_ref, w_uk_ref, pos_ref, len_ref, cache_ref, w_uv_ref, out_ref,
                   q32, query, cache, w_uv, scores, packed, cache_sems, w_sem, *, chunks, log_scale):
    requests=len_ref.shape[0]
    heads=w_uk_ref.shape[0]
    slots=cache.shape[1]
    width=slots//chunks
    def fetch(j):
        at=pl.ds(j*width,width)
        return pltpu.make_async_copy(cache_ref.at[:,at], cache.at[pl.ds(0,LAT+ROPE),at], cache_sems.at[j])
    for j in range(chunks): fetch(j).start()
    w_copy=pltpu.make_async_copy(w_uv_ref,w_uv,w_sem)
    w_copy.start()
    q32[...]=q_ref[...].astype(jnp.float32)
    cache[LAT+ROPE:,:]=jnp.zeros((cache.shape[0]-LAT-ROPE,slots),jnp.bfloat16)
    lane=lax.broadcasted_iota(jnp.int32,(requests,128),1)
    for h in range(heads):
        nope=q32[pl.ds(h,requests,stride=ROWS),:].astype(jnp.bfloat16)
        latent=jnp.dot(nope,w_uk_ref[h],preferred_element_type=jnp.float32).astype(jnp.bfloat16)
        rope=q32[pl.ds(16+h%8,requests,stride=ROWS),:]
        if h>=8: rope=pltpu.roll(rope,64,1)
        rope=jnp.where(lane<ROPE,rope,0.0).astype(jnp.bfloat16)
        query[h*requests:(h+1)*requests,:LAT]=latent
        query[h*requests:(h+1)*requests,LAT:]=rope
    rows=heads*requests
    top=None
    for j in range(chunks):
        fetch(j).wait()
        at=slice(j*width,(j+1)*width)
        s=jnp.dot(query[...],cache[:,at],preferred_element_type=jnp.float32)
        bias=jnp.where(pos_ref[:,at]<len_ref[...],0.0,NEG)
        s=(s.reshape(heads,requests,width)*log_scale+bias[None]).reshape(rows,width)
        scores[:,at]=s
        m=jnp.max(s,axis=1,keepdims=True)
        top=m if top is None else jnp.maximum(top,m)
    mass=None
    acc=None
    for j in range(chunks):
        at=slice(j*width,(j+1)*width)
        p=jnp.exp2(scores[:,at]-top)
        pb=p.astype(jnp.bfloat16)
        l=jnp.sum(p,axis=1,keepdims=True)
        o=lax.dot_general(pb,cache[:LAT,at],(((1,),(1,)),((),())),preferred_element_type=jnp.float32)
        mass=l if mass is None else mass+l
        acc=o if acc is None else acc+o
    w_copy.wait()
    high=acc.astype(jnp.bfloat16)
    low=(acc-high.astype(jnp.float32)).astype(jnp.bfloat16)
    peak_tile=jnp.zeros((requests,128),jnp.float32)
    mass_tile=jnp.zeros((requests,128),jnp.float32)
    packed[...]=jnp.zeros(packed.shape,jnp.float32)
    for h in range(heads):
        r=slice(h*requests,(h+1)*requests)
        both=jnp.concatenate([high[r],low[r]],axis=0)
        v=jnp.dot(both,w_uv[h],preferred_element_type=jnp.float32)
        packed[pl.ds(h,requests,stride=ROWS),:]=v[:requests]+v[requests:]
        peak_tile=jnp.where(lane==h,top[r],peak_tile)
        mass_tile=jnp.where(lane==h,mass[r],mass_tile)
    def parts(x,n):
        got=[]
        for _ in range(n):
            t=x.astype(jnp.bfloat16).astype(jnp.float32)
            got.append(t); x=x-t
        return got
    stats=None
    for k,t in enumerate(parts(peak_tile,3)+parts(mass_tile,2)):
        t=pltpu.roll(t,16*k,1) if k else t
        stats=t if stats is None else stats+t
    packed[pl.ds(heads,requests,stride=ROWS),:]=stats
    out_ref[...]=packed[...].astype(jnp.bfloat16)


def segment(q,w_uk,pos,lens,cacheT,w_uv,chunks=4):
    heads=w_uk.shape[0]; requests=lens.shape[0]; slots=cacheT.shape[1]
    rows=heads*requests
    vm=pl.BlockSpec(memory_space=pltpu.VMEM); hbm=pl.BlockSpec(memory_space=pltpu.HBM)
    return pl.pallas_call(
        functools.partial(segment_kernel,chunks=chunks,log_scale=(NOPE+ROPE)**-0.5*math.log2(math.e)),
        out_shape=jax.ShapeDtypeStruct((requests*ROWS,128),jnp.bfloat16),
        in_specs=[vm,vm,vm,vm,hbm,hbm], out_specs=vm,
        scratch_shapes=[pltpu.VMEM((requests*ROWS,128),jnp.float32),pltpu.VMEM((rows,640),jnp.bfloat16),
            pltpu.VMEM((640,slots),jnp.bfloat16),pltpu.VMEM(w_uv.shape,jnp.bfloat16),
            pltpu.VMEM((rows,slots),jnp.float32),pltpu.VMEM((requests*ROWS,128),jnp.float32),
            pltpu.SemaphoreType.DMA((chunks,)),pltpu.SemaphoreType.DMA],
        compiler_params=pltpu.CompilerParams(vmem_limit_bytes=50 * 1024 * 1024),
        name="segment",
    )(q,w_uk,pos,lens,cacheT,w_uv)


def combine_kernel(got_ref, tail_ref, tail_stats_ref, out_ref, got32, *, heads, sources):
    got32[...] = got_ref[...].astype(jnp.float32)
    stats = got32[pl.ds(heads, sources, stride=ROWS), :]

    def part(first, count):
        terms = [pltpu.roll(stats, (LANES - 16 * k) % LANES, 1) if k else stats for k in range(first, first + count)]
        return sum(terms[1:], terms[0])

    peak = part(0, 3)
    mass = part(3, 2)
    tail_peak = tail_stats_ref[0:1, :]
    tail_mass = tail_stats_ref[1:2, :]
    highest = jnp.maximum(jnp.max(peak, axis=0, keepdims=True), tail_peak)
    factor = jnp.exp2(peak - highest)
    tail_factor = jnp.exp2(tail_peak - highest)
    total = jnp.sum(factor * mass, axis=0, keepdims=True) + tail_factor * tail_mass
    lane = lax.broadcasted_iota(jnp.int32, total.shape, 1)
    total = jnp.where(lane < heads, total, 1.0)
    share = jnp.concatenate(
        [
            factor / total,
            jnp.broadcast_to(tail_factor / total, (8, LANES)),
            jnp.zeros((LANES - sources - 8, LANES), jnp.float32),
        ],
        axis=0,
    )
    share = share.T[:heads]
    value = tail_ref[...] * share[:, sources : sources + 1]
    for s in range(sources):
        value = value + got32[s * ROWS : s * ROWS + heads, :] * share[:, s : s + 1]
    value = value.astype(jnp.bfloat16)
    for s in range(sources):
        out_ref[s * heads : (s + 1) * heads, :] = value


def combine(got, tail, tail_stats, sources):
    heads = tail.shape[0]
    return pl.pallas_call(
        functools.partial(combine_kernel, heads=heads, sources=sources),
        out_shape=jax.ShapeDtypeStruct((sources * heads, LANES), jnp.bfloat16),
        in_specs=[pl.BlockSpec(memory_space=pltpu.VMEM)] * 3,
        out_specs=pl.BlockSpec(memory_space=pltpu.VMEM),
        scratch_shapes=[pltpu.VMEM((sources * ROWS, LANES), jnp.float32)],
        compiler_params=pltpu.CompilerParams(vmem_limit_bytes=8 * 1024 * 1024),
        name="combine",
    )(got, tail, tail_stats)


def output_kernel(values_ref, w_ref, out_ref, values32, flat, *, heads, requests):
    values32[...] = values_ref[...].astype(jnp.float32)
    for h in range(heads):
        flat[:, h * LANES : (h + 1) * LANES] = values32[pl.ds(h, requests, stride=heads), :].astype(
            jnp.bfloat16
        )
    out_ref[...] = lax.dot_general(
        flat[...], w_ref[...], (((1,), (1,)), ((), ())), preferred_element_type=jnp.float32
    )


def output_product(values, w_out_t, requests):
    heads = values.shape[0] // requests
    return pl.pallas_call(
        functools.partial(output_kernel, heads=heads, requests=requests),
        out_shape=jax.ShapeDtypeStruct((requests, w_out_t.shape[0]), jnp.float32),
        in_specs=[pl.BlockSpec(memory_space=pltpu.VMEM)] * 2,
        out_specs=pl.BlockSpec(memory_space=pltpu.VMEM),
        scratch_shapes=[
            pltpu.VMEM(values.shape, jnp.float32),
            pltpu.VMEM((requests, heads * LANES), jnp.bfloat16),
        ],
        compiler_params=pltpu.CompilerParams(vmem_limit_bytes=8 * 1024 * 1024),
        name="output_product",
    )(values, w_out_t)


def spread(block, axis):
    count = lax.axis_size(axis)
    return lax.all_to_all(
        jnp.broadcast_to(block[None], (count, *block.shape)), axis, 0, 0, tiled=True
    )


def tail_part(q_nope, q_rope, w_uk, w_uv, suffix, suffix_len):
    latent = jnp.einsum("hn,hnc->hc", q_nope, w_uk, preferred_element_type=jnp.float32)
    query = jnp.concatenate([latent.astype(jnp.bfloat16), q_rope], axis=1)
    scores = jnp.einsum("hc,tc->ht", query, suffix, preferred_element_type=jnp.float32)
    scores = scores * ((NOPE + ROPE) ** -0.5)
    visible = (jnp.arange(suffix.shape[0], dtype=jnp.int32) < suffix_len)[None, :]
    peak = jnp.max(jnp.where(visible, scores, NEG), axis=1)
    weights = jnp.where(visible, jnp.exp(scores - peak[:, None]), 0.0).astype(jnp.bfloat16)
    mass = jnp.sum(weights, axis=1, dtype=jnp.float32)
    weighted = jnp.einsum("ht,tc->hc", weights, suffix[:, :LAT], preferred_element_type=jnp.float32)
    high = weighted.astype(jnp.bfloat16)
    low = (weighted - high.astype(jnp.float32)).astype(jnp.bfloat16)
    value = jnp.einsum(
        "phc,hcv->phv", jnp.stack([high, low]), w_uv, preferred_element_type=jnp.float32
    ).sum(axis=0)
    stats = jnp.pad(jnp.stack([peak * LOG2E, mass]), ((0, 6), (0, LANES - peak.shape[0])))
    return value, stats


def on_device(
    q_nope,
    q_rope,
    w_uk,
    w_uv,
    w_out,
    prefix_cache,
    block_table,
    prefix_len,
    suffix_cache,
    suffix_len,
):
    requests = prefix_len.shape[0]
    heads = w_uk.shape[0]
    half = heads // 2
    rope_pairs = jnp.concatenate([q_rope[0, :half], q_rope[0, half:]], axis=1)
    raw = spread(jnp.concatenate([q_nope[0], rope_pairs], axis=0), "ctx")
    positions = (
        block_table[:, None] * BLOCK + jnp.arange(BLOCK, dtype=jnp.int32)[None, :]
    ).reshape(1, -1)
    packed = segment(
        raw.reshape(requests * ROWS, LANES),
        w_uk,
        positions,
        prefix_len[:, None],
        prefix_cache.T,
        w_uv,
    )
    got = lax.all_to_all(packed.reshape(requests, ROWS, LANES), "ctx", 0, 0, tiled=True)
    tail, tail_stats = tail_part(
        q_nope[0], q_rope[0], w_uk, w_uv, suffix_cache[0], suffix_len
    )
    values = combine(got.reshape(requests * ROWS, LANES), tail, tail_stats, requests)
    every = lax.all_to_all(values.reshape(requests, heads, LANES), "ctx", 0, 0, tiled=True)
    partial = output_product(every.reshape(requests * heads, LANES), w_out.T, requests)
    tp = lax.axis_size("tp")
    pieces = lax.all_to_all(
        partial.reshape(tp, requests // tp, -1), "tp", 0, 0, tiled=True
    )
    return pieces.sum(axis=0).astype(jnp.bfloat16)


def solution(mesh):
    placed = (
        P("ctx", "tp", None),
        P("ctx", "tp", None),
        P("tp", None, None),
        P("tp", None, None),
        P("tp", "ctx"),
        P("ctx", None),
        P("ctx"),
        P(),
        P("ctx", None, None),
        P("ctx"),
    )
    return jax.shard_map(
        on_device, mesh=mesh, in_specs=placed, out_specs=P("tp", "ctx"), check_vma=False
    )
```

time: 129 us -> 77.2 us (0.60)
  waiting for transfers between devices: 45.8 us -> 13.7 us
  matrix products: 16.3 us -> 4.41 us
  Pallas kernels: 0 us -> 11.4 us
  other arithmetic: 11.8 us -> 2.31 us
  local copies, waits for them, and re-layouts: 7.07 us -> 1.79 us
  blocking collectives: 28.7 us -> 25.8 us
    all_to_all x2, waiting for transfers between devices: 45.8 us -> 13.7 us  [the longest x1 7.96 us: on_device(): lax.all_to_all(packed.reshape(requests, ROWS, LANES), 'ctx', 0, 0, tiled=...]
    dot_general x7 -> x4, matrix products: 16.3 us -> 4.41 us  [the longest x1 1.98 us: tail_part(): jnp.einsum('hn,hnc->hc', q_nope, w_uk, preferred_element_type=jnp.float32)]
    pallas_call x0 -> x3, Pallas kernels: none -> 11.4 us  [the longest x1 10.6 us: segment(): pl.pallas_call(functools.partial(segment_kernel, chunks=chunks, log_scale...]
    unnamed x10, local copies, waits for them, and re-layouts: 4.04 us -> 0.02 us
    reduce_sum x5 -> x2, other arithmetic: 3.85 us -> 0.79 us  [the longest x1 0.6 us: on_device(): return pieces.sum(axis=0).astype(jnp.bfloat16)]
    all_to_all x2, blocking collectives: 28.7 us -> 25.8 us  [the longest x1 13 us: on_device(): lax.all_to_all(partial.reshape(tp, requests // tp, -1), 'tp', 0, 0, tiled...]
    broadcast_in_dim x3 -> x0, other arithmetic: 2.08 us -> none  [sent_to_all(): jnp.broadcast_to(value[None], (length, *value.shape))]
    concatenate x1, other arithmetic: 2.55 us -> 0.76 us  [on_device(): raw = spread(jnp.concatenate([q_nope[0], rope_pairs], axis=0), 'ctx')]
  transfers between devices with their start and end apart: 2 -> 2, of which waited for: 2 -> 2; matrix products, arithmetic and copies ran while one was open for 2% -> 7% of each run, Pallas kernels for 0% -> 0%
where the time goes in v2:
time: 77.2 us; the launch traced here: 76.8 us
  blocking collectives  25.8 us (33%)
  starting transfers between devices  16.6 us (22%)
  waiting for transfers between devices  13.7 us (18%)
  Pallas kernels  11.4 us (15%)
  matrix products  4.41 us (6%)
  other arithmetic  2.31 us (3%)
  local copies, waits for them, and re-layouts  1.79 us (2%)
  between operations  0.8 us (1%)
    all_to_all x1, blocking collectives, on_device(): lax.all_to_all(partial.reshape(tp, requests // tp, -1), 'tp', 0, 0, tiled...  13 us
    all_to_all x1, blocking collectives, on_device(): lax.all_to_all(values.reshape(requests, heads, LANES), 'ctx', 0, 0, tiled...  12.8 us
    all_to_all x1, starting transfers between devices, spread(): lax.all_to_all(jnp.broadcast_to(block[None], (count, *block.shape)), axis...  11.9 us
    pallas_call x1, Pallas kernels, segment(): pl.pallas_call(functools.partial(segment_kernel, chunks=chunks, log_scale...  10.6 us
    all_to_all x1, waiting for transfers between devices, on_device(): lax.all_to_all(packed.reshape(requests, ROWS, LANES), 'ctx', 0, 0, tiled=...  7.96 us
    all_to_all x1, waiting for transfers between devices, spread(): lax.all_to_all(jnp.broadcast_to(block[None], (count, *block.shape)), axis...  5.71 us
    all_to_all x1, starting transfers between devices, on_device(): lax.all_to_all(packed.reshape(requests, ROWS, LANES), 'ctx', 0, 0, tiled=...  4.75 us
    dot_general x1, matrix products, tail_part(): jnp.einsum('hn,hnc->hc', q_nope, w_uk, preferred_element_type=jnp.float32)  1.98 us
  transfers between devices with their start and end apart: 2, of which 2 were waited for; matrix products, arithmetic and copies ran while one was open for 7% of the time, Pallas kernels for 0%

profile of v2, /device:TPU:1, one launch (start us, length us, event | category | flops | bytes accessed | tf_op | source)
XLA Modules:
  0.0 76.8 jit_solution(10055940122228581062)
XLA Ops:
  0.0 0.0 copy-start.3
  0.0 0.0 copy-start
  0.0 0.0 copy-start.2
  0.0 0.0 copy-start.4
  0.0 0.9 %slice_bitcast_fusion.1 = (bf16[8,64]{1,0:T(8,128)(2,1)S(1)}, bf16[8,64]{1,0:T(8,128)(2,1)S(1)}) fusion(bf16[1,16,64]{2,1,0:T(8,128)(2,1)} %param.11), kind=kLoop, calls=%fused_computation.24 | loop fusion | bytes 4096 | tf_op jit(solution)/shard_map/squeeze | solution.py:225
  0.9 0.8 maximum_maximum_fusion
  1.6 0.7 broadcast_in_dim.31
  2.3 11.9 %all-to-all-start = ((bf16[32,24,128]{2,1,0:T(8,128)(2,1)}), bf16[32,24,128]{2,1,0:T(8,128)(2,1)S(1)}, u32[]{:S(2)}, u32[]{:S(2)}) async-start(bf16[32,24,128]{2,1,0:T(8,128)(2,1)} %broadcast_in_dim.31), calls=%async_computation | async-start | bytes 393216 | tf_op jit(solution)/shard_map/all_to_all | solution.py:186
  14.2 0.7 broadcast_multiply_fusion
  14.9 0.1 iota_add_fusion
  15.6 2.0 %fusion.7 = bf16[16,1,512]{2,1,0:T(2,128)(2,1)S(1)} fusion(bf16[16,128,512]{2,1,0:T(8,128)(2,1)} %w_uk_ref.1, bf16[16,128,1]{1,0,2:T(8,128)(2,1)} %bitcast.43), kind=kOutput, calls=%fused_computation.16 | convolution fusion | flops 2097152 | bytes 2117632 | tf_op jit(solution)/shard_map/hn,hnc->hc/dot_general | solution.py:192
  17.6 0.0 copy-done.3
  17.6 0.0 copy-done.2
  17.6 0.3 select_reduce_fusion
  17.9 0.2 convert_reduce_fusion
  18.1 0.1 add.28.pos_ref
  18.2 0.0 copy-done.4
  18.2 0.1 copy.11.len_ref
  18.3 0.2 convert_bitcast_fusion
  18.5 5.7 %all-to-all-done = bf16[32,24,128]{2,1,0:T(8,128)(2,1)S(1)} async-done(((bf16[32,24,128]{2,1,0:T(8,128)(2,1)}), bf16[32,24,128]{2,1,0:T(8,128)(2,1)S(1)}, u32[]{:S(2)}, u32[]{:S(2)}) %all-to-all-start) | async-done | bytes 196640 | tf_op jit(solution)/shard_map/all_to_all | solution.py:186
  24.2 0.0 copy-done
  24.2 10.6 %segment.1 = bf16[768,128]{1,0:T(8,128)(2,1)} custom-call(bf16[768,128]{1,0:T(8,128)(2,1)S(1)} %bitcast.36, bf16[16,128,512]{2,1,0:T(8,128)(2,1)S(1)} %copy-done, s32[1,4096]{1,0:T(1,128)S(1)} %add.28.pos_ref, s32[32,1]{1,0:T(8,128)S(1)} %copy.11.len_ref, bf16[576,4096]{1,0:T(8,128)(2,1)} %bitcast.39, bf16[16,512,128]{2,1,0:T(8,128)(2,1)} %w_uv_ref.1), custom_call_target="tpu_custom_call" | custom-call | tf_op jit(solution)/shard_map/segment/pallas_call | solution.py:96
  34.8 0.0 copy-start.1
  34.8 4.7 %all-to-all-start.1 = ((bf16[32,24,128]{2,1,0:T(8,128)(2,1)}), bf16[32,24,128]{2,1,0:T(8,128)(2,1)S(1)}, u32[]{:S(2)}, u32[]{:S(2)}) async-start(bf16[32,24,128]{2,1,0:T(8,128)(2,1)} %bitcast.6), calls=%async_computation.1 | async-start | bytes 393216 | tf_op jit(solution)/shard_map/all_to_all | solution.py:238
  39.6 2.0 %convolution_reduce_fusion.tail_ref = f32[16,128]{1,0:T(8,128)S(1)} fusion(bf16[16,512,128]{2,1,0:T(8,128)(2,1)} %w_uv_ref.1, bf16[2,16,512]{2,1,0:T(8,128)(2,1)S(1)} %pad_maximum_fusion), kind=kOutput, calls=%fused_computation.1 | convolution fusion | flops 4196352 | bytes 2138112 | tf_op jit(solution)/shard_map/phc,hcv->phv/dot_general | solution.py:203
  41.6 8.0 %all-to-all-done.1 = bf16[32,24,128]{2,1,0:T(8,128)(2,1)S(1)} async-done(((bf16[32,24,128]{2,1,0:T(8,128)(2,1)}), bf16[32,24,128]{2,1,0:T(8,128)(2,1)S(1)}, u32[]{:S(2)}, u32[]{:S(2)}) %all-to-all-start.1) | async-done | bytes 196640 | tf_op jit(solution)/shard_map/all_to_all | solution.py:238
  49.5 0.4 combine.1
  49.9 12.8 %all_to_all.20 = bf16[32,16,128]{2,1,0:T(8,128)(2,1)S(1)} all-to-all(bf16[32,16,128]{2,1,0:T(8,128)(2,1)S(1)} %bitcast.38), channel_id=1, replica_groups=mesh['ctx'=32,'tp'=8] {'ctx'}, dimensions={0} | all-to-all | bytes 262144 | tf_op jit(solution)/shard_map/all_to_all | solution.py:243
  62.8 0.0 copy-done.1
  62.8 0.4 output_product.1
  63.2 13.0 %all_to_all.21 = f32[8,4,224]{2,1,0:T(4,128)S(1)} all-to-all(f32[8,4,224]{2,1,0:T(4,128)S(1)} %reshape.63), channel_id=1, replica_groups=mesh['ctx'=32,'tp'=8] {'tp'}, dimensions={0} | all-to-all | bytes 57344 | tf_op jit(solution)/shard_map/all_to_all | solution.py:246
  76.2 0.6 reduce_sum.29
  (6 shorter events, 0.1 us)
Async XLA Ops:
  0.0 17.6 %copy-start.3 = (bf16[1,16,64]{2,1,0:T(8,128)(2,1)S(1)}, bf16[1,16,64]{2,1,0:T(8,128)(2,1)}, u32[]{:S(2)}) copy-start(bf16[1,16,64]{2,1,0:T(8,128)(2,1)} %param.11) | copy-start | bytes 6148
  0.0 24.2 %copy-start = (bf16[16,128,512]{2,1,0:T(8,128)(2,1)S(1)}, bf16[16,128,512]{2,1,0:T(8,128)(2,1)}, u32[]{:S(2)}) copy-start(bf16[16,128,512]{2,1,0:T(8,128)(2,1)} %w_uk_ref.1) | copy-start | bytes 6291460
  0.0 17.6 %copy-start.2 = (bf16[1,256,576]{1,2,0:T(8,128)(2,1)S(1)}, bf16[1,256,576]{1,2,0:T(8,128)(2,1)}, u32[]{:S(2)}) copy-start(bf16[1,256,576]{1,2,0:T(8,128)(2,1)} %param.18) | copy-start | bytes 884740
  0.0 18.2 %copy-start.4 = (s32[32]{0:T(128)S(1)}, s32[32]{0:T(128)}, u32[]{:S(2)}) copy-start(s32[32]{0:T(128)} %param.17) | copy-start | bytes 388
  2.3 21.8 %all-to-all-start = ((bf16[32,24,128]{2,1,0:T(8,128)(2,1)}), bf16[32,24,128]{2,1,0:T(8,128)(2,1)S(1)}, u32[]{:S(2)}, u32[]{:S(2)}) async-start(bf16[32,24,128]{2,1,0:T(8,128)(2,1)} %broadcast_in_dim.31), calls=%async_computation | async-start | bytes 393216 | tf_op jit(solution)/shard_map/all_to_all | solution.py:186
  34.8 28.0 %copy-start.1 = (bf16[2048,224]{0,1:T(8,128)(2,1)S(1)}, bf16[2048,224]{0,1:T(8,128)(2,1)}, u32[]{:S(2)}) copy-start(bf16[2048,224]{0,1:T(8,128)(2,1)} %param.14) | copy-start | bytes 2752516
  34.8 14.7 %all-to-all-start.1 = ((bf16[32,24,128]{2,1,0:T(8,128)(2,1)}), bf16[32,24,128]{2,1,0:T(8,128)(2,1)S(1)}, u32[]{:S(2)}, u32[]{:S(2)}) async-start(bf16[32,24,128]{2,1,0:T(8,128)(2,1)} %bitcast.6), calls=%async_computation.1 | async-start | bytes 393216 | tf_op jit(solution)/shard_map/all_to_all | solution.py:238

commit v3 on v2

v3 whole, which is shorter than its diff:
```python
import functools
import math

import jax
import jax.numpy as jnp
from jax import lax
from jax.experimental import pallas as pl
from jax.experimental.pallas import tpu as pltpu
from jax.sharding import PartitionSpec as P

LAT = 512
ROPE = 64
NOPE = 128
BLOCK = 64
LANES = 128
ROWS = 24
NEG = -1e30
WHOLE_VMEM = 60 * 1024 * 1024
SCALE = (NOPE + ROPE) ** -0.5 * math.log2(math.e)


def segment_kernel(
    q_ref,
    w_uk_ref,
    pos_ref,
    len_ref,
    cache_ref,
    w_uv_ref,
    out_ref,
    q32,
    query,
    cache,
    w_uv,
    packed,
    cache_sems,
    w_sem,
    *,
    pieces,
):
    requests = len_ref.shape[0]
    heads = w_uk_ref.shape[0]
    half = heads // 2
    rows = heads * requests
    width = cache.shape[1] // sum(pieces)
    firsts = [sum(pieces[:k]) for k in range(len(pieces))]

    def piece(k):
        at = pl.ds(firsts[k] * width, pieces[k] * width)
        return pltpu.make_async_copy(
            cache_ref.at[:, at], cache.at[pl.ds(0, LAT + ROPE), at], cache_sems.at[k]
        )

    for k in range(len(pieces)):
        piece(k).start()
    w_copy = pltpu.make_async_copy(w_uv_ref, w_uv, w_sem)
    w_copy.start()

    q32[...] = q_ref[...].astype(jnp.float32)
    cache[LAT + ROPE :, :] = jnp.zeros((cache.shape[0] - LAT - ROPE, cache.shape[1]), jnp.bfloat16)
    lane = lax.broadcasted_iota(jnp.int32, (requests, LANES), 1)
    for h in range(heads):
        at = slice(h * requests, (h + 1) * requests)
        nope = q32[pl.ds(h, requests, stride=ROWS), :].astype(jnp.bfloat16)
        latent = jnp.dot(nope, w_uk_ref[h], preferred_element_type=jnp.float32)
        rope = q32[pl.ds(heads + h % half, requests, stride=ROWS), :]
        if h >= half:
            rope = pltpu.roll(rope, LANES - ROPE, 1)
        query[at, :LAT] = latent.astype(jnp.bfloat16)
        query[at, LAT:] = jnp.where(lane < ROPE, rope, 0.0).astype(jnp.bfloat16)

    peak = mass = total = None

    def take(at, scores):
        nonlocal peak, mass, total
        highest = jnp.max(scores, axis=1, keepdims=True)
        if peak is not None:
            highest = jnp.maximum(peak, highest)
        weights = jnp.exp2(scores - highest)
        part = jnp.sum(weights, axis=1, keepdims=True)
        values = lax.dot_general(
            weights.astype(jnp.bfloat16),
            cache[:LAT, at],
            (((1,), (1,)), ((), ())),
            preferred_element_type=jnp.float32,
        )
        if peak is None:
            mass, total = part, values
        else:
            keep = jnp.exp2(peak - highest)
            mass, total = mass * keep + part, total * keep + values
        peak = highest

    waiting = None
    for j in range(sum(pieces)):
        if j in firsts:
            piece(firsts.index(j)).wait()
            if j == firsts[-1]:
                w_copy.wait()
        at = slice(j * width, (j + 1) * width)
        scores = jnp.dot(query[...], cache[:, at], preferred_element_type=jnp.float32)
        hidden = jnp.where(pos_ref[:, at] < len_ref[...], 0.0, NEG)
        scores = scores.reshape(heads, requests, width) * SCALE + hidden[None]
        if waiting is not None:
            take(*waiting)
        waiting = (at, scores.reshape(rows, width))
    take(*waiting)

    high = total.astype(jnp.bfloat16)
    low = (total - high.astype(jnp.float32)).astype(jnp.bfloat16)
    peaks = jnp.zeros((requests, LANES), jnp.float32)
    masses = jnp.zeros((requests, LANES), jnp.float32)
    packed[...] = jnp.zeros(packed.shape, jnp.float32)
    for h in range(heads):
        at = slice(h * requests, (h + 1) * requests)
        both = jnp.concatenate([high[at], low[at]], axis=0)
        value = jnp.dot(both, w_uv[h], preferred_element_type=jnp.float32)
        packed[pl.ds(h, requests, stride=ROWS), :] = value[:requests] + value[requests:]
        peaks = jnp.where(lane == h, peak[at], peaks)
        masses = jnp.where(lane == h, mass[at], masses)

    def terms(x, count):
        found = []
        for _ in range(count):
            term = x.astype(jnp.bfloat16).astype(jnp.float32)
            found.append(term)
            x = x - term
        return found

    stats = None
    for k, term in enumerate(terms(peaks, 3) + terms(masses, 2)):
        term = pltpu.roll(term, 16 * k, 1) if k else term
        stats = term if stats is None else stats + term
    packed[pl.ds(heads, requests, stride=ROWS), :] = stats
    out_ref[...] = packed[...].astype(jnp.bfloat16)


def segment(q, w_uk, positions, lens, cache_t, w_uv, pieces=(2, 6)):
    heads = w_uk.shape[0]
    requests = lens.shape[0]
    vmem = pl.BlockSpec(memory_space=pltpu.VMEM)
    hbm = pl.BlockSpec(memory_space=pltpu.HBM)
    return pl.pallas_call(
        functools.partial(segment_kernel, pieces=pieces),
        out_shape=jax.ShapeDtypeStruct((requests * ROWS, LANES), jnp.bfloat16),
        in_specs=[vmem, vmem, vmem, vmem, hbm, hbm],
        out_specs=vmem,
        scratch_shapes=[
            pltpu.VMEM((requests * ROWS, LANES), jnp.float32),
            pltpu.VMEM((heads * requests, LAT + LANES), jnp.bfloat16),
            pltpu.VMEM((LAT + LANES, cache_t.shape[1]), jnp.bfloat16),
            pltpu.VMEM(w_uv.shape, jnp.bfloat16),
            pltpu.VMEM((requests * ROWS, LANES), jnp.float32),
            pltpu.SemaphoreType.DMA((len(pieces),)),
            pltpu.SemaphoreType.DMA,
        ],
        compiler_params=pltpu.CompilerParams(vmem_limit_bytes=50 * 1024 * 1024),
        name="segment",
    )(q, w_uk, positions, lens, cache_t, w_uv)


def start_fetch(pairs, sems):
    copies = [pltpu.make_async_copy(a, b, sems.at[k]) for k, (a, b) in enumerate(pairs)]
    for copy in copies:
        copy.start()
    return copies


def fetch(pairs, sems):
    for copy in start_fetch(pairs, sems):
        copy.wait()


def pack_kernel(q_nope_hbm, q_rope_hbm, out_ref, q_nope_ref, q_rope_ref, sems):
    fetch([(q_nope_hbm, q_nope_ref), (q_rope_hbm, q_rope_ref)], sems)
    rope = q_rope_ref[...].astype(jnp.float32)
    half = rope.shape[0] // 2
    pairs = jnp.concatenate([rope[:half], rope[half:]], axis=1)
    block = jnp.concatenate([q_nope_ref[...].astype(jnp.float32), pairs], axis=0)
    block = block.astype(jnp.bfloat16)
    out_ref[...] = jnp.broadcast_to(block[None], out_ref.shape)


def pack(q_nope, q_rope, count):
    return pl.pallas_call(
        pack_kernel,
        out_shape=jax.ShapeDtypeStruct((count, ROWS, LANES), jnp.bfloat16),
        in_specs=[pl.BlockSpec(memory_space=pltpu.HBM)] * 2,
        out_specs=pl.BlockSpec(memory_space=pltpu.VMEM),
        scratch_shapes=[
            pltpu.VMEM(q_nope.shape, q_nope.dtype),
            pltpu.VMEM(q_rope.shape, q_rope.dtype),
            pltpu.SemaphoreType.DMA((2,)),
        ],
        compiler_params=pltpu.CompilerParams(vmem_limit_bytes=WHOLE_VMEM),
        name="pack",
    )(q_nope, q_rope)


def tail_kernel(
    q_nope_hbm,
    q_rope_hbm,
    w_uk_hbm,
    w_uv_hbm,
    suffix_hbm,
    len_ref,
    out_ref,
    stats_ref,
    q_nope_ref,
    q_rope_ref,
    w_uk_ref,
    suffix_ref,
    w_uv,
    sems,
):
    copies = start_fetch(
        [
            (q_nope_hbm, q_nope_ref),
            (q_rope_hbm, q_rope_ref),
            (w_uk_hbm, w_uk_ref),
            (suffix_hbm, suffix_ref),
            (w_uv_hbm, w_uv),
        ],
        sems,
    )
    for copy in copies[:-1]:
        copy.wait()
    heads = q_nope_ref.shape[0]

    def spread_heads(x):
        row = lax.broadcasted_iota(jnp.int32, x.shape, 0) % heads
        return jnp.concatenate(
            [jnp.where(row == h, x, 0.0).astype(jnp.bfloat16) for h in range(heads)], axis=1
        )

    latent = jnp.dot(
        spread_heads(q_nope_ref[...].astype(jnp.float32)),
        w_uk_ref[...].reshape(-1, LAT),
        preferred_element_type=jnp.float32,
    ).astype(jnp.bfloat16)
    scores = jnp.dot(latent, suffix_ref[:LAT, :], preferred_element_type=jnp.float32)
    scores = scores + jnp.dot(
        q_rope_ref[...], suffix_ref[LAT:, :], preferred_element_type=jnp.float32
    )
    slot = lax.broadcasted_iota(jnp.int32, scores.shape, 1)
    scores = scores * SCALE + jnp.where(slot < len_ref[0], 0.0, NEG)
    peak = jnp.max(scores, axis=1, keepdims=True)
    weights = jnp.exp2(scores - peak)
    mass = jnp.sum(weights, axis=1, keepdims=True)
    weighted = lax.dot_general(
        weights.astype(jnp.bfloat16),
        suffix_ref[:LAT, :],
        (((1,), (1,)), ((), ())),
        preferred_element_type=jnp.float32,
    )
    high = weighted.astype(jnp.bfloat16).astype(jnp.float32)
    both = spread_heads(jnp.concatenate([high, weighted - high], axis=0))
    copies[-1].wait()
    value = jnp.dot(both, w_uv[...].reshape(-1, LANES), preferred_element_type=jnp.float32)
    out_ref[...] = value[:heads] + value[heads:]
    row = lax.broadcasted_iota(jnp.int32, (heads, LANES), 0)
    lane = lax.broadcasted_iota(jnp.int32, (heads, LANES), 1)
    stats_ref[0:1, :] = jnp.sum(jnp.where(row == lane, peak, 0.0), axis=0, keepdims=True)
    stats_ref[1:2, :] = jnp.sum(jnp.where(row == lane, mass, 0.0), axis=0, keepdims=True)


def tail_part(q_nope, q_rope, w_uk, w_uv, suffix_t, suffix_len):
    vmem = pl.BlockSpec(memory_space=pltpu.VMEM)
    return pl.pallas_call(
        tail_kernel,
        out_shape=(
            jax.ShapeDtypeStruct((q_nope.shape[0], LANES), jnp.float32),
            jax.ShapeDtypeStruct((2, LANES), jnp.float32),
        ),
        in_specs=[pl.BlockSpec(memory_space=pltpu.HBM)] * 5
        + [pl.BlockSpec(memory_space=pltpu.SMEM)],
        out_specs=(vmem, vmem),
        scratch_shapes=[
            pltpu.VMEM(x.shape, x.dtype) for x in (q_nope, q_rope, w_uk, suffix_t, w_uv)
        ]
        + [pltpu.SemaphoreType.DMA((5,))],
        compiler_params=pltpu.CompilerParams(vmem_limit_bytes=WHOLE_VMEM),
        name="tail",
    )(q_nope, q_rope, w_uk, w_uv, suffix_t, suffix_len)


def combine_kernel(got_ref, tail_ref, tail_stats_ref, out_ref, got32, *, heads, sources):
    got32[...] = got_ref[...].astype(jnp.float32)
    stats = got32[pl.ds(heads, sources, stride=ROWS), :]

    def part(first, count):
        terms = [pltpu.roll(stats, (LANES - 16 * k) % LANES, 1) if k else stats for k in range(first, first + count)]
        return sum(terms[1:], terms[0])

    peak = part(0, 3)
    mass = part(3, 2)
    tail_peak = tail_stats_ref[0:1, :]
    tail_mass = tail_stats_ref[1:2, :]
    highest = jnp.maximum(jnp.max(peak, axis=0, keepdims=True), tail_peak)
    factor = jnp.exp2(peak - highest)
    tail_factor = jnp.exp2(tail_peak - highest)
    total = jnp.sum(factor * mass, axis=0, keepdims=True) + tail_factor * tail_mass
    lane = lax.broadcasted_iota(jnp.int32, total.shape, 1)
    total = jnp.where(lane < heads, total, 1.0)
    share = jnp.concatenate(
        [
            factor / total,
            jnp.broadcast_to(tail_factor / total, (8, LANES)),
            jnp.zeros((LANES - sources - 8, LANES), jnp.float32),
        ],
        axis=0,
    )
    share = share.T[:heads]
    value = tail_ref[...] * share[:, sources : sources + 1]
    for s in range(sources):
        value = value + got32[s * ROWS : s * ROWS + heads, :] * share[:, s : s + 1]
    value = value.astype(jnp.bfloat16)
    for s in range(sources):
        out_ref[s * heads : (s + 1) * heads, :] = value


def combine(got, tail, tail_stats, sources):
    heads = tail.shape[0]
    return pl.pallas_call(
        functools.partial(combine_kernel, heads=heads, sources=sources),
        out_shape=jax.ShapeDtypeStruct((sources * heads, LANES), jnp.bfloat16),
        in_specs=[pl.BlockSpec(memory_space=pltpu.VMEM)] * 3,
        out_specs=pl.BlockSpec(memory_space=pltpu.VMEM),
        scratch_shapes=[pltpu.VMEM((sources * ROWS, LANES), jnp.float32)],
        compiler_params=pltpu.CompilerParams(vmem_limit_bytes=8 * 1024 * 1024),
        name="combine",
    )(got, tail, tail_stats)


def output_kernel(values_ref, w_ref, out_ref, values32, flat, *, heads, requests):
    values32[...] = values_ref[...].astype(jnp.float32)
    for h in range(heads):
        flat[:, h * LANES : (h + 1) * LANES] = values32[pl.ds(h, requests, stride=heads), :].astype(
            jnp.bfloat16
        )
    out_ref[...] = lax.dot_general(
        flat[...], w_ref[...], (((1,), (1,)), ((), ())), preferred_element_type=jnp.float32
    )


def output_product(values, w_out_t, requests):
    heads = values.shape[0] // requests
    return pl.pallas_call(
        functools.partial(output_kernel, heads=heads, requests=requests),
        out_shape=jax.ShapeDtypeStruct((requests, w_out_t.shape[0]), jnp.float32),
        in_specs=[pl.BlockSpec(memory_space=pltpu.VMEM)] * 2,
        out_specs=pl.BlockSpec(memory_space=pltpu.VMEM),
        scratch_shapes=[
            pltpu.VMEM(values.shape, jnp.float32),
            pltpu.VMEM((requests, heads * LANES), jnp.bfloat16),
        ],
        compiler_params=pltpu.CompilerParams(vmem_limit_bytes=8 * 1024 * 1024),
        name="output_product",
    )(values, w_out_t)


def on_device(
    q_nope,
    q_rope,
    w_uk,
    w_uv,
    w_out,
    prefix_cache,
    block_table,
    prefix_len,
    suffix_cache,
    suffix_len,
):
    requests = prefix_len.shape[0]
    heads = w_uk.shape[0]
    raw = lax.all_to_all(pack(q_nope[0], q_rope[0], requests), "ctx", 0, 0, tiled=True)
    tail, tail_stats = tail_part(
        q_nope[0], q_rope[0], w_uk, w_uv, suffix_cache[0].T, suffix_len
    )
    positions = (
        block_table[:, None] * BLOCK + jnp.arange(BLOCK, dtype=jnp.int32)[None, :]
    ).reshape(1, -1)
    raw, tail, tail_stats = lax.optimization_barrier((raw, tail, tail_stats))
    packed = segment(
        raw.reshape(requests * ROWS, LANES),
        w_uk,
        positions,
        prefix_len[:, None],
        prefix_cache.T,
        w_uv,
    )
    got = lax.all_to_all(packed.reshape(requests, ROWS, LANES), "ctx", 0, 0, tiled=True)
    values = combine(got.reshape(requests * ROWS, LANES), tail, tail_stats, requests)
    every = lax.all_to_all(values.reshape(requests, heads, LANES), "ctx", 0, 0, tiled=True)
    partial = output_product(every.reshape(requests * heads, LANES), w_out.T, requests)
    tp = lax.axis_size("tp")
    pieces = lax.all_to_all(
        partial.reshape(tp, requests // tp, -1), "tp", 0, 0, tiled=True
    )
    return pieces.sum(axis=0).astype(jnp.bfloat16)


def solution(mesh):
    placed = (
        P("ctx", "tp", None),
        P("ctx", "tp", None),
        P("tp", None, None),
        P("tp", None, None),
        P("tp", "ctx"),
        P("ctx", None),
        P("ctx"),
        P(),
        P("ctx", None, None),
        P("ctx"),
    )
    return jax.shard_map(
        on_device, mesh=mesh, in_specs=placed, out_specs=P("tp", "ctx"), check_vma=False
    )
```

time: 77.2 us -> 74.9 us (0.970)
  blocking collectives: 25.8 us -> 40.8 us
  waiting for transfers between devices: 13.7 us -> 3.9 us
  starting transfers between devices: 16.6 us -> 11.9 us
  matrix products: 4.41 us -> 0 us
  Pallas kernels: 11.4 us -> 15 us
  other arithmetic: 2.31 us -> 1.33 us
  local copies, waits for them, and re-layouts: 1.79 us -> 0.87 us
    all_to_all x0 -> x1, blocking collectives: none -> 15 us  [on_device(): lax.all_to_all(packed.reshape(requests, ROWS, LANES), 'ctx', 0, 0, tiled=...]
    all_to_all x2 -> x1, waiting for transfers between devices: 13.7 us -> 3.9 us  [on_device(): lax.all_to_all(pack(q_nope[0], q_rope[0], requests), 'ctx', 0, 0, tiled=T...]
    all_to_all x2 -> x1, starting transfers between devices: 16.6 us -> 11.9 us  [on_device(): lax.all_to_all(pack(q_nope[0], q_rope[0], requests), 'ctx', 0, 0, tiled=T...]
    dot_general x4 -> x0, matrix products: 4.41 us -> none  [the longest x1 1.98 us: tail_part(): jnp.einsum('hn,hnc->hc', q_nope, w_uk, preferred_element_type=jnp.float32)]
    pallas_call x1 -> x3, Pallas kernels: 10.6 us -> 14.2 us  [the longest x1 8.92 us: segment(): pl.pallas_call(functools.partial(segment_kernel, pieces=pieces), out_shap...]
    squeeze x1 -> x0, local copies, waits for them, and re-layouts: 0.85 us -> none  [on_device(): rope_pairs = jnp.concatenate([q_rope[0, :half], q_rope[0, half:]], axis=1)]
  transfers between devices with their start and end apart: 2 -> 1, of which waited for: 2 -> 1; matrix products, arithmetic and copies ran while one was open for 7% -> 2% of each run, Pallas kernels for 0% -> 5%
where the time goes in v3:
time: 74.9 us; the launch traced here: 74.5 us
  blocking collectives  40.8 us (54%)
  Pallas kernels  15 us (20%)
  starting transfers between devices  11.9 us (16%)
  waiting for transfers between devices  3.9 us (5%)
  other arithmetic  1.33 us (2%)
  local copies, waits for them, and re-layouts  0.87 us (1%)
    all_to_all x1, blocking collectives, on_device(): lax.all_to_all(packed.reshape(requests, ROWS, LANES), 'ctx', 0, 0, tiled=...  15 us
    all_to_all x1, blocking collectives, on_device(): lax.all_to_all(values.reshape(requests, heads, LANES), 'ctx', 0, 0, tiled...  13 us
    all_to_all x1, blocking collectives, on_device(): lax.all_to_all(partial.reshape(tp, requests // tp, -1), 'tp', 0, 0, tiled...  12.8 us
    all_to_all x1, starting transfers between devices, on_device(): lax.all_to_all(pack(q_nope[0], q_rope[0], requests), 'ctx', 0, 0, tiled=T...  11.9 us
    pallas_call x1, Pallas kernels, segment(): pl.pallas_call(functools.partial(segment_kernel, pieces=pieces), out_shap...  8.92 us
    all_to_all x1, waiting for transfers between devices, on_device(): lax.all_to_all(pack(q_nope[0], q_rope[0], requests), 'ctx', 0, 0, tiled=T...  3.9 us
    pallas_call x1, Pallas kernels, tail_part(): pl.pallas_call(tail_kernel, out_shape=(jax.ShapeDtypeStruct((q_nope.shape...  3.85 us
  transfers between devices with their start and end apart: 1, of which 1 were waited for; matrix products, arithmetic and copies ran while one was open for 2% of the time, Pallas kernels for 5%

profile of v3, /device:TPU:1, one launch (start us, length us, event | category | flops | bytes accessed | tf_op | source)
XLA Modules:
  0.0 74.5 jit_solution(10092987245450012404)
XLA Ops:
  0.0 1.5 %pack.1 = bf16[32,24,128]{2,1,0:T(8,128)(2,1)} custom-call(bf16[16,128]{1,0:T(8,128)(2,1)} %bitcast.21, bf16[16,64]{1,0:T(8,128)(2,1)} %bitcast.23), custom_call_target="tpu_custom_call" | custom-call | tf_op jit(solution)/shard_map/pack/pallas_call | solution.py:184
  1.5 11.9 %all-to-all-start = ((bf16[32,24,128]{2,1,0:T(8,128)(2,1)}), bf16[32,24,128]{2,1,0:T(8,128)(2,1)S(1)}, u32[]{:S(2)}, u32[]{:S(2)}) async-start(bf16[32,24,128]{2,1,0:T(8,128)(2,1)} %pack.1), calls=%async_computation | async-start | bytes 393216 | tf_op jit(solution)/shard_map/all_to_all | solution.py:375
  14.0 0.7 broadcast_multiply_fusion
  14.7 0.1 iota_add_fusion
  14.7 0.1 add.26.pos_ref
  14.8 0.7 copy.11.len_ref
  15.6 0.0 copy-start
  15.6 3.8 %tail.1 = (f32[16,128]{1,0:T(8,128)}, f32[2,128]{1,0:T(2,128)}) custom-call(bf16[16,128]{1,0:T(8,128)(2,1)} %bitcast.22, bf16[16,64]{1,0:T(8,128)(2,1)} %bitcast.24, bf16[16,128,512]{2,1,0:T(8,128)(2,1)} %w_uk_ref.1, bf16[16,512,128]{2,1,0:T(8,128)(2,1)} %w_uv_ref.1, bf16[576,256]{1,0:T(8,128)(2,1)} %bitcast.20, s32[1]{0:T(128)S(6)} %copy.12.len_ref), custom_call_target="tpu_custom_call" | custom-call | tf_op jit(solution)/shard_map/tail/pallas_call | solution.py:268
  19.4 3.9 %all-to-all-done = bf16[32,24,128]{2,1,0:T(8,128)(2,1)S(1)} async-done(((bf16[32,24,128]{2,1,0:T(8,128)(2,1)}), bf16[32,24,128]{2,1,0:T(8,128)(2,1)S(1)}, u32[]{:S(2)}, u32[]{:S(2)}) %all-to-all-start) | async-done | bytes 196640 | tf_op jit(solution)/shard_map/all_to_all | solution.py:375
  23.3 0.0 copy-done
  23.3 0.0 copy-start.2
  23.3 0.0 copy-start.3
  23.3 0.0 copy-start.1
  23.3 8.9 %segment.1 = bf16[768,128]{1,0:T(8,128)(2,1)S(1)} custom-call(bf16[768,128]{1,0:T(8,128)(2,1)S(1)} %bitcast.15, bf16[16,128,512]{2,1,0:T(8,128)(2,1)S(1)} %copy-done, s32[1,4096]{1,0:T(1,128)S(1)} %add.26.pos_ref, s32[32,1]{1,0:T(8,128)S(1)} %copy.11.len_ref, bf16[576,4096]{1,0:T(8,128)(2,1)} %bitcast.19, bf16[16,512,128]{2,1,0:T(8,128)(2,1)} %w_uv_ref.1), custom_call_target="tpu_custom_call" | custom-call | tf_op jit(solution)/shard_map/segment/pallas_call | solution.py:142
  32.3 15.0 %all_to_all.20 = bf16[32,24,128]{2,1,0:T(8,128)(2,1)S(1)} all-to-all(bf16[32,24,128]{2,1,0:T(8,128)(2,1)S(1)} %bitcast.16), channel_id=1, replica_groups=mesh['ctx'=32,'tp'=8] {'ctx'}, dimensions={0} | all-to-all | bytes 393216 | tf_op jit(solution)/shard_map/all_to_all | solution.py:391
  47.3 0.0 copy-done.2
  47.3 0.0 copy-done.3
  47.3 0.4 combine.1
  47.7 13.0 %all_to_all.21 = bf16[32,16,128]{2,1,0:T(8,128)(2,1)S(1)} all-to-all(bf16[32,16,128]{2,1,0:T(8,128)(2,1)S(1)} %bitcast.18), channel_id=1, replica_groups=mesh['ctx'=32,'tp'=8] {'ctx'}, dimensions={0} | all-to-all | bytes 262144 | tf_op jit(solution)/shard_map/all_to_all | solution.py:393
  60.7 0.0 copy-done.1
  60.7 0.4 output_product.1
  61.2 12.8 %all_to_all.22 = f32[8,4,224]{2,1,0:T(4,128)S(1)} all-to-all(f32[8,4,224]{2,1,0:T(4,128)S(1)} %reshape.48), channel_id=1, replica_groups=mesh['ctx'=32,'tp'=8] {'tp'}, dimensions={0} | all-to-all | bytes 57344 | tf_op jit(solution)/shard_map/all_to_all | solution.py:396
  73.9 0.6 reduce_sum.9
  (1 shorter events, 0.0 us)
Async XLA Ops:
  1.5 21.8 %all-to-all-start = ((bf16[32,24,128]{2,1,0:T(8,128)(2,1)}), bf16[32,24,128]{2,1,0:T(8,128)(2,1)S(1)}, u32[]{:S(2)}, u32[]{:S(2)}) async-start(bf16[32,24,128]{2,1,0:T(8,128)(2,1)} %pack.1), calls=%async_computation | async-start | bytes 393216 | tf_op jit(solution)/shard_map/all_to_all | solution.py:375
  15.6 7.8 %copy-start = (bf16[16,128,512]{2,1,0:T(8,128)(2,1)S(1)}, bf16[16,128,512]{2,1,0:T(8,128)(2,1)}, u32[]{:S(2)}) copy-start(bf16[16,128,512]{2,1,0:T(8,128)(2,1)} %w_uk_ref.1) | copy-start | bytes 6291460
  23.3 24.0 %copy-start.2 = (f32[16,128]{1,0:T(8,128)S(1)}, f32[16,128]{1,0:T(8,128)}, u32[]{:S(2)}) copy-start(f32[16,128]{1,0:T(8,128)} %get-tuple-element.13.tail_ref) | copy-start | bytes 24580
  23.3 24.0 %copy-start.3 = (f32[2,128]{1,0:T(2,128)S(1)}, f32[2,128]{1,0:T(2,128)}, u32[]{:S(2)}) copy-start(f32[2,128]{1,0:T(2,128)} %get-tuple-element.14.tail_stats_ref) | copy-start | bytes 3076
  23.3 37.4 %copy-start.1 = (bf16[2048,224]{0,1:T(8,128)(2,1)S(1)}, bf16[2048,224]{0,1:T(8,128)(2,1)}, u32[]{:S(2)}) copy-start(bf16[2048,224]{0,1:T(8,128)(2,1)} %param.14) | copy-start | bytes 2752516

commit v4 on v3

--- a/solution.py
+++ b/solution.py
@@ -15,6 +15,8 @@
 LANES = 128
 ROWS = 24
 NEG = -1e30
+CTX_FIRST = 18
+TP_FIRST = 4
 WHOLE_VMEM = 60 * 1024 * 1024
 SCALE = (NOPE + ROPE) ** -0.5 * math.log2(math.e)
 
@@ -76,7 +78,7 @@
         if peak is not None:
             highest = jnp.maximum(peak, highest)
         weights = jnp.exp2(scores - highest)
-        part = jnp.sum(weights, axis=1, keepdims=True)
+        part = sum(weights[:, k : k + LANES] for k in range(0, width, LANES))
         values = lax.dot_general(
             weights.astype(jnp.bfloat16),
             cache[:LAT, at],
@@ -104,6 +106,7 @@
             take(*waiting)
         waiting = (at, scores.reshape(rows, width))
     take(*waiting)
+    mass = jnp.sum(mass, axis=1, keepdims=True)
 
     high = total.astype(jnp.bfloat16)
     low = (total - high.astype(jnp.float32)).astype(jnp.bfloat16)
@@ -331,21 +334,22 @@
     )(got, tail, tail_stats)
 
 
-def output_kernel(values_ref, w_ref, out_ref, values32, flat, *, heads, requests):
+def output_kernel(values_ref, w_ref, out_ref, values32, flat, *, heads, requests, first):
     values32[...] = values_ref[...].astype(jnp.float32)
     for h in range(heads):
-        flat[:, h * LANES : (h + 1) * LANES] = values32[pl.ds(h, requests, stride=heads), :].astype(
-            jnp.bfloat16
-        )
-    out_ref[...] = lax.dot_general(
+        value = values32[pl.ds(h, requests, stride=heads), :]
+        flat[:, h * LANES : (h + 1) * LANES] = pltpu.roll(value, CTX_FIRST, 0).astype(jnp.bfloat16)
+    product = lax.dot_general(
         flat[...], w_ref[...], (((1,), (1,)), ((), ())), preferred_element_type=jnp.float32
     )
-
-
-def output_product(values, w_out_t, requests):
+    out_ref[: requests - first, :] = product[first:]
+    out_ref[requests - first :, :] = product[:first]
+
+
+def output_product(values, w_out_t, requests, first):
     heads = values.shape[0] // requests
     return pl.pallas_call(
-        functools.partial(output_kernel, heads=heads, requests=requests),
+        functools.partial(output_kernel, heads=heads, requests=requests, first=first),
         out_shape=jax.ShapeDtypeStruct((requests, w_out_t.shape[0]), jnp.float32),
         in_specs=[pl.BlockSpec(memory_space=pltpu.VMEM)] * 2,
         out_specs=pl.BlockSpec(memory_space=pltpu.VMEM),
@@ -356,6 +360,12 @@
         compiler_params=pltpu.CompilerParams(vmem_limit_bytes=8 * 1024 * 1024),
         name="output_product",
     )(values, w_out_t)
+
+
+def exchange(value, axis, first):
+    count = lax.axis_size(axis)
+    order = [[(k + first) % count for k in range(count)]]
+    return lax.all_to_all(value, axis, 0, 0, axis_index_groups=order, tiled=True)
 
 
 def on_device(
@@ -372,7 +382,7 @@
 ):
     requests = prefix_len.shape[0]
     heads = w_uk.shape[0]
-    raw = lax.all_to_all(pack(q_nope[0], q_rope[0], requests), "ctx", 0, 0, tiled=True)
+    raw = exchange(pack(q_nope[0], q_rope[0], requests), "ctx", CTX_FIRST)
     tail, tail_stats = tail_part(
         q_nope[0], q_rope[0], w_uk, w_uv, suffix_cache[0].T, suffix_len
     )
@@ -384,18 +394,17 @@
         raw.reshape(requests * ROWS, LANES),
         w_uk,
         positions,
-        prefix_len[:, None],
+        jnp.roll(prefix_len, -CTX_FIRST)[:, None],
         prefix_cache.T,
         w_uv,
     )
-    got = lax.all_to_all(packed.reshape(requests, ROWS, LANES), "ctx", 0, 0, tiled=True)
+    got = exchange(packed.reshape(requests, ROWS, LANES), "ctx", CTX_FIRST)
     values = combine(got.reshape(requests * ROWS, LANES), tail, tail_stats, requests)
-    every = lax.all_to_all(values.reshape(requests, heads, LANES), "ctx", 0, 0, tiled=True)
-    partial = output_product(every.reshape(requests * heads, LANES), w_out.T, requests)
+    every = exchange(values.reshape(requests, heads, LANES), "ctx", CTX_FIRST)
     tp = lax.axis_size("tp")
-    pieces = lax.all_to_all(
-        partial.reshape(tp, requests // tp, -1), "tp", 0, 0, tiled=True
-    )
+    first = TP_FIRST * (requests // tp)
+    partial = output_product(every.reshape(requests * heads, LANES), w_out.T, requests, first)
+    pieces = exchange(partial.reshape(tp, requests // tp, -1), "tp", TP_FIRST)
     return pieces.sum(axis=0).astype(jnp.bfloat16)
 
 

time: 74.9 us -> 68.7 us (0.917)
  blocking collectives: 40.8 us -> 36 us
  waiting for transfers between devices: 3.9 us -> 0.01 us
  starting transfers between devices: 11.9 us -> 13.9 us
    all_to_all x3, blocking collectives: 40.8 us -> 36 us  [exchange(): lax.all_to_all(value, axis, 0, 0, axis_index_groups=order, tiled=True)]
    all_to_all x1, waiting for transfers between devices: 3.9 us -> 0.01 us  [exchange(): lax.all_to_all(value, axis, 0, 0, axis_index_groups=order, tiled=True)]
    all_to_all x1, starting transfers between devices: 11.9 us -> 13.9 us  [exchange(): lax.all_to_all(value, axis, 0, 0, axis_index_groups=order, tiled=True)]
  transfers between devices with their start and end apart: 1 -> 1, of which waited for: 1 -> 0; matrix products, arithmetic and copies ran while one was open for 2% -> 3% of each run, Pallas kernels for 5% -> 6%
where the time goes in v4:
time: 68.7 us; the launch traced here: 68.4 us
  blocking collectives  36 us (52%)
  Pallas kernels  14.7 us (21%)
  starting transfers between devices  13.9 us (20%)
  other arithmetic  2.06 us (3%)
  local copies, waits for them, and re-layouts  0.95 us (1%)
  between operations  0.77 us (1%)
    all_to_all x3, blocking collectives, exchange(): lax.all_to_all(value, axis, 0, 0, axis_index_groups=order, tiled=True)  36 us
    all_to_all x1, starting transfers between devices, exchange(): lax.all_to_all(value, axis, 0, 0, axis_index_groups=order, tiled=True)  13.9 us
    pallas_call x1, Pallas kernels, segment(): pl.pallas_call(functools.partial(segment_kernel, pieces=pieces), out_shap...  8.59 us
    pallas_call x1, Pallas kernels, tail_part(): pl.pallas_call(tail_kernel, out_shape=(jax.ShapeDtypeStruct((q_nope.shape...  3.85 us
    pallas_call x1, Pallas kernels, pack(): pl.pallas_call(pack_kernel, out_shape=jax.ShapeDtypeStruct((count, ROWS,...  1.47 us
  transfers between devices with their start and end apart: 1, of which 0 were waited for; matrix products, arithmetic and copies ran while one was open for 3% of the time, Pallas kernels for 6%

profile of v4, /device:TPU:1, one launch (start us, length us, event | category | flops | bytes accessed | tf_op | source)
XLA Modules:
  0.0 68.4 jit_solution(1829828496124513292)
XLA Ops:
  0.0 1.5 %pack.1 = bf16[32,24,128]{2,1,0:T(8,128)(2,1)} custom-call(bf16[16,128]{1,0:T(8,128)(2,1)} %bitcast.23, bf16[16,64]{1,0:T(8,128)(2,1)} %bitcast.25), custom_call_target="tpu_custom_call" | custom-call | tf_op jit(solution)/shard_map/pack/pallas_call | solution.py:187
  1.5 13.9 %all-to-all-start = ((bf16[32,24,128]{2,1,0:T(8,128)(2,1)}), bf16[32,24,128]{2,1,0:T(8,128)(2,1)S(1)}, u32[]{:S(2)}, u32[]{:S(2)}) async-start(bf16[32,24,128]{2,1,0:T(8,128)(2,1)} %pack.1), calls=%async_computation | async-start | bytes 393216 | tf_op jit(solution)/shard_map/all_to_all | solution.py:368
  15.4 0.7 broadcast_multiply_fusion
  16.7 0.1 iota_add_fusion
  16.8 0.1 add.26.pos_ref
  16.9 0.7 %slice.8 = s32[14]{0:T(128)S(1)} slice(s32[32]{0:T(128)} %param.17), slice={[18:32]} | slice | bytes 112 | tf_op jit(solution)/shard_map/jit(_roll_static)/slice | solution.py:397
  17.6 0.7 %add_bitcast_fusion = s32[32,1]{0,1:T(1,128)S(1)} fusion(s32[18]{0:T(128)} %bitcast.27, s32[14]{0:T(128)S(1)} %slice.8), kind=kLoop, calls=%fused_computation.1 | loop fusion | flops 32 | bytes 256 | tf_op jit(solution)/shard_map/broadcast_in_dim | solution.py:397
  18.3 0.1 copy.11.len_ref
  18.4 0.0 copy-start
  18.4 3.8 %tail.1 = (f32[16,128]{1,0:T(8,128)}, f32[2,128]{1,0:T(2,128)}) custom-call(bf16[16,128]{1,0:T(8,128)(2,1)} %bitcast.24, bf16[16,64]{1,0:T(8,128)(2,1)} %bitcast.26, bf16[16,128,512]{2,1,0:T(8,128)(2,1)} %w_uk_ref.1, bf16[16,512,128]{2,1,0:T(8,128)(2,1)} %w_uv_ref.1, bf16[576,256]{1,0:T(8,128)(2,1)} %bitcast.22, s32[1]{0:T(128)S(6)} %copy.12.len_ref), custom_call_target="tpu_custom_call" | custom-call | tf_op jit(solution)/shard_map/tail/pallas_call | solution.py:271
  22.3 0.0 all-to-all-done
  22.3 0.0 copy-done
  22.3 0.0 copy-start.2
  22.3 0.0 copy-start.3
  22.3 0.0 copy-start.1
  22.3 8.6 %segment.1 = bf16[768,128]{1,0:T(8,128)(2,1)S(1)} custom-call(bf16[768,128]{1,0:T(8,128)(2,1)S(1)} %bitcast.17, bf16[16,128,512]{2,1,0:T(8,128)(2,1)S(1)} %copy-done, s32[1,4096]{1,0:T(1,128)S(1)} %add.26.pos_ref, s32[32,1]{1,0:T(8,128)S(1)} %copy.11.len_ref, bf16[576,4096]{1,0:T(8,128)(2,1)} %bitcast.21, bf16[16,512,128]{2,1,0:T(8,128)(2,1)} %w_uv_ref.1), custom_call_target="tpu_custom_call" | custom-call | tf_op jit(solution)/shard_map/segment/pallas_call | solution.py:145
  30.9 13.1 %all_to_all.20 = bf16[32,24,128]{2,1,0:T(8,128)(2,1)S(1)} all-to-all(bf16[32,24,128]{2,1,0:T(8,128)(2,1)S(1)} %bitcast.18), channel_id=1, replica_groups={{144,152,160,168,176,184,192,200,208,216,224,232,240,248,0,8,16,24,32,4..., dimensions={0} | all-to-all | bytes 393216 | tf_op jit(solution)/shard_map/all_to_all | solution.py:368
  44.0 0.0 copy-done.2
  44.0 0.0 copy-done.3
  44.0 0.4 combine.1
  44.5 12.1 %all_to_all.21 = bf16[32,16,128]{2,1,0:T(8,128)(2,1)S(1)} all-to-all(bf16[32,16,128]{2,1,0:T(8,128)(2,1)S(1)} %bitcast.20), channel_id=1, replica_groups={{144,152,160,168,176,184,192,200,208,216,224,232,240,248,0,8,16,24,32,4..., dimensions={0} | all-to-all | bytes 262144 | tf_op jit(solution)/shard_map/all_to_all | solution.py:368
  56.5 0.0 copy-done.1
  56.5 0.4 output_product.1
  56.9 10.8 %all_to_all.22 = f32[8,4,224]{2,1,0:T(4,128)S(1)} all-to-all(f32[8,4,224]{2,1,0:T(4,128)S(1)} %reshape.48), channel_id=1, replica_groups={{4,5,6,7,0,1,2,3},{12,13,14,15,8,9,10,11},{20,21,22,23,16,17,18,19},{28..., dimensions={0} | all-to-all | bytes 57344 | tf_op jit(solution)/shard_map/all_to_all | solution.py:368
  67.8 0.6 reduce_sum.9
  (1 shorter events, 0.0 us)
Async XLA Ops:
  1.5 20.8 %all-to-all-start = ((bf16[32,24,128]{2,1,0:T(8,128)(2,1)}), bf16[32,24,128]{2,1,0:T(8,128)(2,1)S(1)}, u32[]{:S(2)}, u32[]{:S(2)}) async-start(bf16[32,24,128]{2,1,0:T(8,128)(2,1)} %pack.1), calls=%async_computation | async-start | bytes 393216 | tf_op jit(solution)/shard_map/all_to_all | solution.py:368
  18.4 3.9 %copy-start = (bf16[16,128,512]{2,1,0:T(8,128)(2,1)S(1)}, bf16[16,128,512]{2,1,0:T(8,128)(2,1)}, u32[]{:S(2)}) copy-start(bf16[16,128,512]{2,1,0:T(8,128)(2,1)} %w_uk_ref.1) | copy-start | bytes 6291460
  22.3 21.7 %copy-start.2 = (f32[16,128]{1,0:T(8,128)S(1)}, f32[16,128]{1,0:T(8,128)}, u32[]{:S(2)}) copy-start(f32[16,128]{1,0:T(8,128)} %get-tuple-element.13.tail_ref) | copy-start | bytes 24580
  22.3 21.7 %copy-start.3 = (f32[2,128]{1,0:T(2,128)S(1)}, f32[2,128]{1,0:T(2,128)}, u32[]{:S(2)}) copy-start(f32[2,128]{1,0:T(2,128)} %get-tuple-element.14.tail_stats_ref) | copy-start | bytes 3076
  22.3 34.2 %copy-start.1 = (bf16[2048,224]{0,1:T(8,128)(2,1)S(1)}, bf16[2048,224]{0,1:T(8,128)(2,1)}, u32[]{:S(2)}) copy-start(bf16[2048,224]{0,1:T(8,128)(2,1)} %param.14) | copy-start | bytes 2752516

commit v5 on v4

--- a/solution.py
+++ b/solution.py
@@ -100,7 +100,7 @@
                 w_copy.wait()
         at = slice(j * width, (j + 1) * width)
         scores = jnp.dot(query[...], cache[:, at], preferred_element_type=jnp.float32)
-        hidden = jnp.where(pos_ref[:, at] < len_ref[...], 0.0, NEG)
+        hidden = jnp.where(pos_ref[:, at] < len_ref[:, :1], 0.0, NEG)
         scores = scores.reshape(heads, requests, width) * SCALE + hidden[None]
         if waiting is not None:
             take(*waiting)
@@ -173,8 +173,29 @@
         copy.wait()
 
 
-def pack_kernel(q_nope_hbm, q_rope_hbm, out_ref, q_nope_ref, q_rope_ref, sems):
-    fetch([(q_nope_hbm, q_nope_ref), (q_rope_hbm, q_rope_ref)], sems)
+def pack_kernel(
+    q_nope_hbm,
+    q_rope_hbm,
+    table_hbm,
+    lens_hbm,
+    out_ref,
+    pos_ref,
+    len_ref,
+    q_nope_ref,
+    q_rope_ref,
+    table,
+    lens,
+    sems,
+):
+    fetch(
+        [
+            (q_nope_hbm, q_nope_ref),
+            (q_rope_hbm, q_rope_ref),
+            (table_hbm, table),
+            (lens_hbm, lens),
+        ],
+        sems,
+    )
     rope = q_rope_ref[...].astype(jnp.float32)
     half = rope.shape[0] // 2
     pairs = jnp.concatenate([rope[:half], rope[half:]], axis=1)
@@ -182,21 +203,39 @@
     block = block.astype(jnp.bfloat16)
     out_ref[...] = jnp.broadcast_to(block[None], out_ref.shape)
 
-
-def pack(q_nope, q_rope, count):
+    lane = lax.broadcasted_iota(jnp.int32, (1, LANES), 1)
+    for k in range(0, table.shape[0], LANES // BLOCK):
+        start = jnp.where(lane < BLOCK, table[k], table[k + 1])
+        pos_ref[:, k * BLOCK : k * BLOCK + LANES] = start * BLOCK + lane % BLOCK
+    count = lens.shape[0]
+    row = lax.broadcasted_iota(jnp.int32, (count, LANES), 0)
+    limit = jnp.zeros((count, LANES), jnp.int32)
+    for r in range(count):
+        limit = jnp.where(row == r, lens[(r + CTX_FIRST) % count], limit)
+    len_ref[...] = limit
+
+
+def pack(q_nope, q_rope, table, lens):
+    count = lens.shape[0]
     return pl.pallas_call(
         pack_kernel,
-        out_shape=jax.ShapeDtypeStruct((count, ROWS, LANES), jnp.bfloat16),
-        in_specs=[pl.BlockSpec(memory_space=pltpu.HBM)] * 2,
-        out_specs=pl.BlockSpec(memory_space=pltpu.VMEM),
+        out_shape=(
+            jax.ShapeDtypeStruct((count, ROWS, LANES), jnp.bfloat16),
+            jax.ShapeDtypeStruct((1, table.shape[0] * BLOCK), jnp.int32),
+            jax.ShapeDtypeStruct((count, LANES), jnp.int32),
+        ),
+        in_specs=[pl.BlockSpec(memory_space=pltpu.HBM)] * 4,
+        out_specs=(pl.BlockSpec(memory_space=pltpu.VMEM),) * 3,
         scratch_shapes=[
             pltpu.VMEM(q_nope.shape, q_nope.dtype),
             pltpu.VMEM(q_rope.shape, q_rope.dtype),
-            pltpu.SemaphoreType.DMA((2,)),
+            pltpu.SMEM(table.shape, table.dtype),
+            pltpu.SMEM(lens.shape, lens.dtype),
+            pltpu.SemaphoreType.DMA((4,)),
         ],
         compiler_params=pltpu.CompilerParams(vmem_limit_bytes=WHOLE_VMEM),
         name="pack",
-    )(q_nope, q_rope)
+    )(q_nope, q_rope, table, lens)
 
 
 def tail_kernel(
@@ -382,19 +421,17 @@
 ):
     requests = prefix_len.shape[0]
     heads = w_uk.shape[0]
-    raw = exchange(pack(q_nope[0], q_rope[0], requests), "ctx", CTX_FIRST)
+    packed_query, positions, lens = pack(q_nope[0], q_rope[0], block_table, prefix_len)
+    raw = exchange(packed_query, "ctx", CTX_FIRST)
     tail, tail_stats = tail_part(
         q_nope[0], q_rope[0], w_uk, w_uv, suffix_cache[0].T, suffix_len
     )
-    positions = (
-        block_table[:, None] * BLOCK + jnp.arange(BLOCK, dtype=jnp.int32)[None, :]
-    ).reshape(1, -1)
     raw, tail, tail_stats = lax.optimization_barrier((raw, tail, tail_stats))
     packed = segment(
         raw.reshape(requests * ROWS, LANES),
         w_uk,
         positions,
-        jnp.roll(prefix_len, -CTX_FIRST)[:, None],
+        lens,
         prefix_cache.T,
         w_uv,
     )

time: 68.7 us -> 67.2 us (0.978)
  other arithmetic: 2.06 us -> 0.6 us
  local copies, waits for them, and re-layouts: 0.95 us -> 0.05 us
    broadcast_in_dim x1 -> x0, other arithmetic: 0.73 us -> none  [on_device(): jnp.roll(prefix_len, -CTX_FIRST)[:, None]]
    slice x1 -> x0, local copies, waits for them, and re-layouts: 0.73 us -> none  [on_device(): jnp.roll(prefix_len, -CTX_FIRST)[:, None]]
  transfers between devices with their start and end apart: 1 -> 1, of which waited for: 0 -> 1; matrix products, arithmetic and copies ran while one was open for 3% -> 0% of each run, Pallas kernels for 6% -> 6%
where the time goes in v5:
time: 67.2 us; the launch traced here: 66.9 us
  blocking collectives  36.1 us (54%)
  Pallas kernels  14.8 us (22%)
  starting transfers between devices  13.9 us (21%)
  between operations  0.76 us (1%)
  waiting for transfers between devices  0.68 us (1%)
    all_to_all x3, blocking collectives, exchange(): lax.all_to_all(value, axis, 0, 0, axis_index_groups=order, tiled=True)  36.1 us
    all_to_all x1, starting transfers between devices, exchange(): lax.all_to_all(value, axis, 0, 0, axis_index_groups=order, tiled=True)  13.9 us
    pallas_call x1, Pallas kernels, segment(): pl.pallas_call(functools.partial(segment_kernel, pieces=pieces), out_shap...  8.58 us
    pallas_call x1, Pallas kernels, tail_part(): pl.pallas_call(tail_kernel, out_shape=(jax.ShapeDtypeStruct((q_nope.shape...  3.84 us
    pallas_call x1, Pallas kernels, pack(): pl.pallas_call(pack_kernel, out_shape=(jax.ShapeDtypeStruct((count, ROWS,...  1.59 us
  transfers between devices with their start and end apart: 1, of which 1 were waited for; matrix products, arithmetic and copies ran while one was open for 0% of the time, Pallas kernels for 6%

profile of v5, /device:TPU:1, one launch (start us, length us, event | category | flops | bytes accessed | tf_op | source)
XLA Modules:
  0.0 66.9 jit_solution(10544266639884534126)
XLA Ops:
  0.0 1.6 %pack.1 = (bf16[32,24,128]{2,1,0:T(8,128)(2,1)}, s32[1,4096]{1,0:T(1,128)}, s32[32,128]{1,0:T(8,128)}) custom-call(bf16[16,128]{1,0:T(8,128)(2,1)} %bitcast.20, bf16[16,64]{1,0:T(8,128)(2,1)} %bitcast.22, s32[64]{0:T(128)} %table_hbm.1, s32[32]{0:T(128)} %lens_hbm.1), custom_call_target="tpu_custom_call" | custom-call | tf_op jit(solution)/shard_map/pack/pallas_call | solution.py:220
  1.6 13.9 %all-to-all-start = ((bf16[32,24,128]{2,1,0:T(8,128)(2,1)}), bf16[32,24,128]{2,1,0:T(8,128)(2,1)S(1)}, u32[]{:S(2)}, u32[]{:S(2)}) async-start(bf16[32,24,128]{2,1,0:T(8,128)(2,1)} %get-tuple-element.13), calls=%async_computation | async-start | bytes 393216 | tf_op jit(solution)/shard_map/all_to_all | solution.py:407
  16.2 0.0 copy-start
  16.2 0.0 copy-start.2
  16.2 0.0 copy-start.3
  16.2 3.8 %tail.1 = (f32[16,128]{1,0:T(8,128)}, f32[2,128]{1,0:T(2,128)}) custom-call(bf16[16,128]{1,0:T(8,128)(2,1)} %bitcast.21, bf16[16,64]{1,0:T(8,128)(2,1)} %bitcast.23, bf16[16,128,512]{2,1,0:T(8,128)(2,1)} %w_uk_ref.1, bf16[16,512,128]{2,1,0:T(8,128)(2,1)} %w_uv_ref.1, bf16[576,256]{1,0:T(8,128)(2,1)} %bitcast.19, s32[1]{0:T(128)S(6)} %copy.11.len_ref), custom_call_target="tpu_custom_call" | custom-call | tf_op jit(solution)/shard_map/tail/pallas_call | solution.py:310
  20.0 0.7 %all-to-all-done = bf16[32,24,128]{2,1,0:T(8,128)(2,1)S(1)} async-done(((bf16[32,24,128]{2,1,0:T(8,128)(2,1)}), bf16[32,24,128]{2,1,0:T(8,128)(2,1)S(1)}, u32[]{:S(2)}, u32[]{:S(2)}) %all-to-all-start) | async-done | bytes 196640 | tf_op jit(solution)/shard_map/all_to_all | solution.py:407
  20.7 0.0 copy-done
  20.7 0.0 copy-done.2
  20.7 0.0 copy-done.3
  20.7 0.0 copy-start.4
  20.7 0.0 copy-start.5
  20.8 0.0 copy-start.1
  20.8 8.6 %segment.1 = bf16[768,128]{1,0:T(8,128)(2,1)S(1)} custom-call(bf16[768,128]{1,0:T(8,128)(2,1)S(1)} %bitcast.14, bf16[16,128,512]{2,1,0:T(8,128)(2,1)S(1)} %copy-done, s32[1,4096]{1,0:T(1,128)S(1)} %copy-done.2, s32[32,128]{1,0:T(8,128)S(1)} %copy-done.3, bf16[576,4096]{1,0:T(8,128)(2,1)} %bitcast.18, bf16[16,512,128]{2,1,0:T(8,128)(2,1)} %w_uv_ref.1), custom_call_target="tpu_custom_call" | custom-call | tf_op jit(solution)/shard_map/segment/pallas_call | solution.py:145
  29.4 13.4 %all_to_all.20 = bf16[32,24,128]{2,1,0:T(8,128)(2,1)S(1)} all-to-all(bf16[32,24,128]{2,1,0:T(8,128)(2,1)S(1)} %bitcast.15), channel_id=1, replica_groups={{144,152,160,168,176,184,192,200,208,216,224,232,240,248,0,8,16,24,32,4..., dimensions={0} | all-to-all | bytes 393216 | tf_op jit(solution)/shard_map/all_to_all | solution.py:407
  42.8 0.0 copy-done.4
  42.8 0.0 copy-done.5
  42.8 0.4 combine.1
  43.2 12.2 %all_to_all.21 = bf16[32,16,128]{2,1,0:T(8,128)(2,1)S(1)} all-to-all(bf16[32,16,128]{2,1,0:T(8,128)(2,1)S(1)} %bitcast.17), channel_id=1, replica_groups={{144,152,160,168,176,184,192,200,208,216,224,232,240,248,0,8,16,24,32,4..., dimensions={0} | all-to-all | bytes 262144 | tf_op jit(solution)/shard_map/all_to_all | solution.py:407
  55.4 0.0 copy-done.1
  55.4 0.4 output_product.1
  55.8 10.5 %all_to_all.22 = f32[8,4,224]{2,1,0:T(4,128)S(1)} all-to-all(f32[8,4,224]{2,1,0:T(4,128)S(1)} %reshape.23), channel_id=1, replica_groups={{4,5,6,7,0,1,2,3},{12,13,14,15,8,9,10,11},{20,21,22,23,16,17,18,19},{28..., dimensions={0} | all-to-all | bytes 57344 | tf_op jit(solution)/shard_map/all_to_all | solution.py:407
  66.3 0.6 reduce_sum.9
  (1 shorter events, 0.0 us)
Async XLA Ops:
  1.6 19.1 %all-to-all-start = ((bf16[32,24,128]{2,1,0:T(8,128)(2,1)}), bf16[32,24,128]{2,1,0:T(8,128)(2,1)S(1)}, u32[]{:S(2)}, u32[]{:S(2)}) async-start(bf16[32,24,128]{2,1,0:T(8,128)(2,1)} %get-tuple-element.13), calls=%async_computation | async-start | bytes 393216 | tf_op jit(solution)/shard_map/all_to_all | solution.py:407
  16.2 4.6 %copy-start = (bf16[16,128,512]{2,1,0:T(8,128)(2,1)S(1)}, bf16[16,128,512]{2,1,0:T(8,128)(2,1)}, u32[]{:S(2)}) copy-start(bf16[16,128,512]{2,1,0:T(8,128)(2,1)} %w_uk_ref.1) | copy-start | bytes 6291460
  16.2 4.5 %copy-start.2 = (s32[1,4096]{1,0:T(1,128)S(1)}, s32[1,4096]{1,0:T(1,128)}, u32[]{:S(2)}) copy-start(s32[1,4096]{1,0:T(1,128)} %get-tuple-element.17.pos_ref) | copy-start | bytes 49156
  16.2 4.5 %copy-start.3 = (s32[32,128]{1,0:T(8,128)S(1)}, s32[32,128]{1,0:T(8,128)}, u32[]{:S(2)}) copy-start(s32[32,128]{1,0:T(8,128)} %get-tuple-element.18.len_ref) | copy-start | bytes 49156
  20.7 22.0 %copy-start.4 = (f32[16,128]{1,0:T(8,128)S(1)}, f32[16,128]{1,0:T(8,128)}, u32[]{:S(2)}) copy-start(f32[16,128]{1,0:T(8,128)} %get-tuple-element.19.tail_ref) | copy-start | bytes 24580
  20.7 22.0 %copy-start.5 = (f32[2,128]{1,0:T(2,128)S(1)}, f32[2,128]{1,0:T(2,128)}, u32[]{:S(2)}) copy-start(f32[2,128]{1,0:T(2,128)} %get-tuple-element.20.tail_stats_ref) | copy-start | bytes 3076
  20.8 34.6 %copy-start.1 = (bf16[2048,224]{0,1:T(8,128)(2,1)S(1)}, bf16[2048,224]{0,1:T(8,128)(2,1)}, u32[]{:S(2)}) copy-start(bf16[2048,224]{0,1:T(8,128)(2,1)} %param.14) | copy-start | bytes 2752516

commit v6 on v5

--- a/solution.py
+++ b/solution.py
@@ -49,7 +49,7 @@
     def piece(k):
         at = pl.ds(firsts[k] * width, pieces[k] * width)
         return pltpu.make_async_copy(
-            cache_ref.at[:, at], cache.at[pl.ds(0, LAT + ROPE), at], cache_sems.at[k]
+            cache_ref.at[:, at], cache.at[:, at], cache_sems.at[k]
         )
 
     for k in range(len(pieces)):
@@ -58,7 +58,6 @@
     w_copy.start()
 
     q32[...] = q_ref[...].astype(jnp.float32)
-    cache[LAT + ROPE :, :] = jnp.zeros((cache.shape[0] - LAT - ROPE, cache.shape[1]), jnp.bfloat16)
     lane = lax.broadcasted_iota(jnp.int32, (requests, LANES), 1)
     for h in range(heads):
         at = slice(h * requests, (h + 1) * requests)
@@ -68,7 +67,7 @@
         if h >= half:
             rope = pltpu.roll(rope, LANES - ROPE, 1)
         query[at, :LAT] = latent.astype(jnp.bfloat16)
-        query[at, LAT:] = jnp.where(lane < ROPE, rope, 0.0).astype(jnp.bfloat16)
+        query[at, LAT:] = rope[:, :ROPE].astype(jnp.bfloat16)
 
     peak = mass = total = None
 
@@ -149,8 +148,8 @@
         out_specs=vmem,
         scratch_shapes=[
             pltpu.VMEM((requests * ROWS, LANES), jnp.float32),
-            pltpu.VMEM((heads * requests, LAT + LANES), jnp.bfloat16),
-            pltpu.VMEM((LAT + LANES, cache_t.shape[1]), jnp.bfloat16),
+            pltpu.VMEM((heads * requests, LAT + ROPE), jnp.bfloat16),
+            pltpu.VMEM(cache_t.shape, jnp.bfloat16),
             pltpu.VMEM(w_uv.shape, jnp.bfloat16),
             pltpu.VMEM((requests * ROWS, LANES), jnp.float32),
             pltpu.SemaphoreType.DMA((len(pieces),)),

time: 67.2 us -> 67.2 us (level)
  no operation moved by 1% of the time
where the time goes in v6:
time: 67.2 us; the launch traced here: 66.9 us
  blocking collectives  36.1 us (54%)
  Pallas kernels  14.8 us (22%)
  starting transfers between devices  13.9 us (21%)
  between operations  0.76 us (1%)
  waiting for transfers between devices  0.68 us (1%)
    all_to_all x3, blocking collectives, exchange(): lax.all_to_all(value, axis, 0, 0, axis_index_groups=order, tiled=True)  36.1 us
    all_to_all x1, starting transfers between devices, exchange(): lax.all_to_all(value, axis, 0, 0, axis_index_groups=order, tiled=True)  13.9 us
    pallas_call x1, Pallas kernels, segment(): pl.pallas_call(functools.partial(segment_kernel, pieces=pieces), out_shap...  8.57 us
    pallas_call x1, Pallas kernels, tail_part(): pl.pallas_call(tail_kernel, out_shape=(jax.ShapeDtypeStruct((q_nope.shape...  3.84 us
    pallas_call x1, Pallas kernels, pack(): pl.pallas_call(pack_kernel, out_shape=(jax.ShapeDtypeStruct((count, ROWS,...  1.59 us
  transfers between devices with their start and end apart: 1, of which 1 were waited for; matrix products, arithmetic and copies ran while one was open for 0% of the time, Pallas kernels for 6%

profile of v6, /device:TPU:1, one launch (start us, length us, event | category | flops | bytes accessed | tf_op | source)
XLA Modules:
  0.0 66.9 jit_solution(17522916958962067887)
XLA Ops:
  0.0 1.6 %pack.1 = (bf16[32,24,128]{2,1,0:T(8,128)(2,1)}, s32[1,4096]{1,0:T(1,128)}, s32[32,128]{1,0:T(8,128)}) custom-call(bf16[16,128]{1,0:T(8,128)(2,1)} %bitcast.20, bf16[16,64]{1,0:T(8,128)(2,1)} %bitcast.22, s32[64]{0:T(128)} %table_hbm.1, s32[32]{0:T(128)} %lens_hbm.1), custom_call_target="tpu_custom_call" | custom-call | tf_op jit(solution)/shard_map/pack/pallas_call | solution.py:219
  1.6 13.9 %all-to-all-start = ((bf16[32,24,128]{2,1,0:T(8,128)(2,1)}), bf16[32,24,128]{2,1,0:T(8,128)(2,1)S(1)}, u32[]{:S(2)}, u32[]{:S(2)}) async-start(bf16[32,24,128]{2,1,0:T(8,128)(2,1)} %get-tuple-element.13), calls=%async_computation | async-start | bytes 393216 | tf_op jit(solution)/shard_map/all_to_all | solution.py:406
  16.2 0.0 copy-start
  16.2 0.0 copy-start.2
  16.2 0.0 copy-start.3
  16.2 3.8 %tail.1 = (f32[16,128]{1,0:T(8,128)}, f32[2,128]{1,0:T(2,128)}) custom-call(bf16[16,128]{1,0:T(8,128)(2,1)} %bitcast.21, bf16[16,64]{1,0:T(8,128)(2,1)} %bitcast.23, bf16[16,128,512]{2,1,0:T(8,128)(2,1)} %w_uk_ref.1, bf16[16,512,128]{2,1,0:T(8,128)(2,1)} %w_uv_ref.1, bf16[576,256]{1,0:T(8,128)(2,1)} %bitcast.19, s32[1]{0:T(128)S(6)} %copy.11.len_ref), custom_call_target="tpu_custom_call" | custom-call | tf_op jit(solution)/shard_map/tail/pallas_call | solution.py:309
  20.0 0.7 %all-to-all-done = bf16[32,24,128]{2,1,0:T(8,128)(2,1)S(1)} async-done(((bf16[32,24,128]{2,1,0:T(8,128)(2,1)}), bf16[32,24,128]{2,1,0:T(8,128)(2,1)S(1)}, u32[]{:S(2)}, u32[]{:S(2)}) %all-to-all-start) | async-done | bytes 196640 | tf_op jit(solution)/shard_map/all_to_all | solution.py:406
  20.7 0.0 copy-done
  20.7 0.0 copy-done.2
  20.7 0.0 copy-done.3
  20.7 0.0 copy-start.4
  20.7 0.0 copy-start.5
  20.8 0.0 copy-start.1
  20.8 8.6 %segment.1 = bf16[768,128]{1,0:T(8,128)(2,1)S(1)} custom-call(bf16[768,128]{1,0:T(8,128)(2,1)S(1)} %bitcast.14, bf16[16,128,512]{2,1,0:T(8,128)(2,1)S(1)} %copy-done, s32[1,4096]{1,0:T(1,128)S(1)} %copy-done.2, s32[32,128]{1,0:T(8,128)S(1)} %copy-done.3, bf16[576,4096]{1,0:T(8,128)(2,1)} %bitcast.18, bf16[16,512,128]{2,1,0:T(8,128)(2,1)} %w_uv_ref.1), custom_call_target="tpu_custom_call" | custom-call | tf_op jit(solution)/shard_map/segment/pallas_call | solution.py:144
  29.3 13.3 %all_to_all.20 = bf16[32,24,128]{2,1,0:T(8,128)(2,1)S(1)} all-to-all(bf16[32,24,128]{2,1,0:T(8,128)(2,1)S(1)} %bitcast.15), channel_id=1, replica_groups={{144,152,160,168,176,184,192,200,208,216,224,232,240,248,0,8,16,24,32,4..., dimensions={0} | all-to-all | bytes 393216 | tf_op jit(solution)/shard_map/all_to_all | solution.py:406
  42.7 0.0 copy-done.4
  42.7 0.0 copy-done.5
  42.7 0.4 combine.1
  43.1 12.3 %all_to_all.21 = bf16[32,16,128]{2,1,0:T(8,128)(2,1)S(1)} all-to-all(bf16[32,16,128]{2,1,0:T(8,128)(2,1)S(1)} %bitcast.17), channel_id=1, replica_groups={{144,152,160,168,176,184,192,200,208,216,224,232,240,248,0,8,16,24,32,4..., dimensions={0} | all-to-all | bytes 262144 | tf_op jit(solution)/shard_map/all_to_all | solution.py:406
  55.4 0.0 copy-done.1
  55.4 0.4 output_product.1
  55.8 10.5 %all_to_all.22 = f32[8,4,224]{2,1,0:T(4,128)S(1)} all-to-all(f32[8,4,224]{2,1,0:T(4,128)S(1)} %reshape.23), channel_id=1, replica_groups={{4,5,6,7,0,1,2,3},{12,13,14,15,8,9,10,11},{20,21,22,23,16,17,18,19},{28..., dimensions={0} | all-to-all | bytes 57344 | tf_op jit(solution)/shard_map/all_to_all | solution.py:406
  66.3 0.6 reduce_sum.9
  (1 shorter events, 0.0 us)
Async XLA Ops:
  1.6 19.1 %all-to-all-start = ((bf16[32,24,128]{2,1,0:T(8,128)(2,1)}), bf16[32,24,128]{2,1,0:T(8,128)(2,1)S(1)}, u32[]{:S(2)}, u32[]{:S(2)}) async-start(bf16[32,24,128]{2,1,0:T(8,128)(2,1)} %get-tuple-element.13), calls=%async_computation | async-start | bytes 393216 | tf_op jit(solution)/shard_map/all_to_all | solution.py:406
  16.2 4.6 %copy-start = (bf16[16,128,512]{2,1,0:T(8,128)(2,1)S(1)}, bf16[16,128,512]{2,1,0:T(8,128)(2,1)}, u32[]{:S(2)}) copy-start(bf16[16,128,512]{2,1,0:T(8,128)(2,1)} %w_uk_ref.1) | copy-start | bytes 6291460
  16.2 4.5 %copy-start.2 = (s32[1,4096]{1,0:T(1,128)S(1)}, s32[1,4096]{1,0:T(1,128)}, u32[]{:S(2)}) copy-start(s32[1,4096]{1,0:T(1,128)} %get-tuple-element.17.pos_ref) | copy-start | bytes 49156
  16.2 4.5 %copy-start.3 = (s32[32,128]{1,0:T(8,128)S(1)}, s32[32,128]{1,0:T(8,128)}, u32[]{:S(2)}) copy-start(s32[32,128]{1,0:T(8,128)} %get-tuple-element.18.len_ref) | copy-start | bytes 49156
  20.7 22.0 %copy-start.4 = (f32[16,128]{1,0:T(8,128)S(1)}, f32[16,128]{1,0:T(8,128)}, u32[]{:S(2)}) copy-start(f32[16,128]{1,0:T(8,128)} %get-tuple-element.19.tail_ref) | copy-start | bytes 24580
  20.7 21.9 %copy-start.5 = (f32[2,128]{1,0:T(2,128)S(1)}, f32[2,128]{1,0:T(2,128)}, u32[]{:S(2)}) copy-start(f32[2,128]{1,0:T(2,128)} %get-tuple-element.20.tail_stats_ref) | copy-start | bytes 3076
  20.8 34.6 %copy-start.1 = (bf16[2048,224]{0,1:T(8,128)(2,1)S(1)}, bf16[2048,224]{0,1:T(8,128)(2,1)}, u32[]{:S(2)}) copy-start(bf16[2048,224]{0,1:T(8,128)(2,1)} %param.14) | copy-start | bytes 2752516
